TPU v7x, 512 devices: a 8x2x16 block of a 8x8x16 slice. The times are simulated.
512 devices in a mesh: img: 2 (over y), sub: 32 (over z, core), rng: 8 (over x).
Axes of the slice: x: 8, y: 2, z: 16, core: 2. Of those that a mesh axis runs over, the one named last changes fastest.
The devices are a block of a 8x8x16 slice.
Arguments:
- image: bfloat16 [2, 128, 128, 4096], P(None, ('img', 'sub'), None, 'rng'), parts along dimension 1, may hold values from -6 to 6
- interp_weights: bfloat16 [4, 2, 2, 2, 128, 128], replicated, may hold values from -0.25 to 0.25
- range_taps: float32 [4, 4], replicated, may hold values from -2 to 2
- range_shifts: int32 [4, 2, 128], replicated, may hold values from -8 to 5
Outputs:
- merged_image: bfloat16 [2, 128, 128, 4096], P(None, ('img', 'sub'), None, 'rng'), parts along dimension 1
There are 2 independent parts, one for each index of `img`. A program takes and returns all parts, laid end to end along the dimension named above; an argument that names none is the same for every part. Nothing has to cross between parts.
All inputs are finite; a program needn't handle non-finite values.
Results may differ from a plain program's by a relative error of at most 0.0095.
Values may be sent and summed in bfloat16 or wider, within the bound.
A program may use at most 64 MiB of HBM per device.

v0:
```python
import math

import jax
import jax.numpy as jnp
from jax import lax
from jax.sharding import PartitionSpec as P

ANGLES = 128
RANGE = 4096
RIM = 8
TAPS = 4
LEVELS = 4


phase_step = 2.0 * math.pi / 64.0


def padded_2(cells, sides, width):
    for axis, dim in sides:
        count = lax.axis_size(axis)
        ends = count - 1
        head = lax.slice_in_dim(cells, 0, width, axis=dim)
        tail = lax.slice_in_dim(cells, cells.shape[dim] - width, cells.shape[dim], axis=dim)
        cells = jnp.concatenate(
            [
                lax.ppermute(tail, axis, [(i, (i + 1) % count) for i in range(ends)]),
                cells,
                lax.ppermute(head, axis, [((i + 1) % count, i) for i in range(ends)]),
            ],
            axis=dim,
        )
    return cells


def from_partner(value, axis, stride):
    mask = 2**stride
    pairs = [(source, source ^ mask) for source in range(lax.axis_size(axis))]
    return lax.ppermute(value, axis, pairs)


def rotate(merged_sum, level_index, half_index, range_start, range_width):
    angle_rows = half_index * ANGLES + jnp.arange(ANGLES, dtype=jnp.int32)
    range_cols = range_start + jnp.arange(range_width, dtype=jnp.int32)
    wrapped = range_cols[None, :] * (angle_rows[:, None] + 1) * (7 + level_index) % 64
    phase = wrapped.astype(jnp.float32) * phase_step
    cosine = jnp.cos(phase)
    sinus = jnp.sin(phase)
    return jnp.stack(
        [
            merged_sum[0] * cosine - merged_sum[1] * sinus,
            merged_sum[0] * sinus + merged_sum[1] * cosine,
        ]
    )


def level_coef(range_taps, range_shifts, level_index, side_index):
    offsets = jnp.arange(2 * RIM + 1, dtype=jnp.int32) - RIM
    tap_ids = jnp.arange(TAPS, dtype=jnp.int32)
    hits = (
        range_shifts[level_index, side_index][:, None, None] + tap_ids[None, :, None]
        == offsets[None, None, :]
    )
    return jnp.einsum("t,ato->ao", range_taps[level_index], hits.astype(jnp.float32))


def interpolate(padded, coef, range_width):
    total = None
    for offset_index in range(2 * RIM + 1):
        term = coef[:, offset_index, None] * padded[
            ..., offset_index : offset_index + range_width
        ].astype(jnp.float32)
        total = term if total is None else total + term
    return total.astype(jnp.bfloat16)


def block_of(weight_pair):
    return jnp.stack(
        [jnp.stack([weight_pair[0], -weight_pair[1]]), jnp.stack([weight_pair[1], weight_pair[0]])]
    )


def combine_sides(lower_rows, upper_rows, weights_level, half_index):
    chosen = lax.dynamic_index_in_dim(weights_level, half_index, 1, keepdims=False)
    merged_sum = None
    for side_index, source in ((0, lower_rows), (1, upper_rows)):
        product = jnp.einsum(
            "xcij,cgjr->xgir",
            block_of(chosen[side_index]),
            source,
            preferred_element_type=jnp.float32,
        )
        merged_sum = product if merged_sum is None else merged_sum + product
    return merged_sum


def on_device(image, interp_weights, range_taps, range_shifts):
    range_width = image.shape[3]
    sub_count = lax.axis_size("sub")
    bit_count = sub_count.bit_length() - 1
    sub_index = lax.axis_index("sub")
    range_start = lax.axis_index("rng") * range_width
    current = padded_2(image, (("rng", 3),), LEVELS * RIM)
    margin = LEVELS * RIM
    for level_index in range(LEVELS):
        bit = level_index % bit_count
        own_half = sub_index // 2**bit % 2
        padded = current
        margin = margin - RIM
        out_width = range_width + 2 * margin
        coef = jnp.where(
            own_half == 0,
            level_coef(range_taps, range_shifts, level_index, 0),
            level_coef(range_taps, range_shifts, level_index, 1),
        )
        own_rows = interpolate(padded, coef, out_width)
        partner = from_partner(own_rows, "sub", bit)
        lower_rows = jnp.where(own_half == 0, own_rows, partner)
        upper_rows = jnp.where(own_half == 0, partner, own_rows)
        merged = combine_sides(lower_rows, upper_rows, interp_weights[level_index], own_half)
        turned = rotate(merged, level_index, own_half, range_start - margin, out_width)
        global_cols = range_start - margin + jnp.arange(out_width, dtype=jnp.int32)
        inside = jnp.logical_and(global_cols >= 0, global_cols < RANGE)
        turned = jnp.where(inside, turned, 0.0)
        current = turned.astype(jnp.bfloat16)
    return current


def solution(mesh):
    return jax.shard_map(
        on_device,
        mesh=mesh,
        in_specs=(P(None, ("img", "sub"), None, "rng"), P(), P(), P()),
        out_specs=P(None, ("img", "sub"), None, "rng"),
        check_vma=False,
    )
```

profile of v0, /device:TPU:65, one launch (start us, length us, event | category | flops | bytes accessed | tf_op | source)
XLA Modules:
  0.0 167.4 jit_solution(8667952678334169549)
XLA Ops:
  0.0 0.0 copy-start
  0.0 1.4 copy.8
  1.4 1.3 collective-permute-start.1
  2.7 4.7 %collective-permute-start = (bf16[2,2,128,32]{2,3,1,0:T(8,128)(2,1)S(1)}, bf16[2,2,128,32]{2,3,1,0:T(8,128)(2,1)S(1)}, u32[]{:S(2)}, u32[]{:S(2)}) collective-permute-start(bf16[2,2,128,32]{2,3,1,0:T(8,128)(2,1)S(1)} %get-tuple-element.49), channel_id=1, source_target_pairs={{0,1},{1,2},{2,3},{3,4},{4,5},{5,6},{6,7},{8,9},{9,10},{10,11},{11... | collective-permute-start | bytes 98312 | tf_op jit(solution)/shard_map/ppermute | solution.py:26
  7.5 0.0 copy-done
  7.5 0.0 copy-start.2
  7.5 0.1 fusion.84
  7.7 0.0 copy-start.1
  8.0 0.2 copy-done.2
  8.2 0.1 copy-done.1
  8.4 0.1 iota_add_fusion.6
  8.5 0.1 iota_add_fusion.4
  8.6 0.1 iota_add_fusion.2
  8.7 0.1 iota_add_fusion
  8.8 1.7 %select_reduce_fusion.6 = (f32[128,17]{1,0:T(8,128)S(1)}, f32[128,17]{1,0:T(8,128)S(1)}, f32[128,17]{1,0:T(8,128)S(1)}, f32[128,17]{1,0:T(8,128)S(1)}, f32[128,1...) fusion(f32[4]{0:T(128)S(1)} %get-tuple-element.169, ...), kind=kLoop, calls=%fused_computation.89 | loop fusion | flops 191488 | bytes 86148
  10.5 0.1 copy.48
  10.5 0.1 copy.53
  10.7 0.1 copy.38
  10.7 0.1 copy.43
  10.9 0.1 copy.28
  10.9 0.1 copy.33
  11.2 0.1 copy.18
  11.2 0.1 copy.23
  11.3 0.0 collective-permute-done.1
  11.3 0.0 collective-permute-done
  11.4 2.5 %add_convert_fusion = bf16[2,2,128,560]{2,3,1,0:T(8,128)(2,1)S(1)} fusion(bf16[2,2,128,576]{2,3,1,0:T(8,128)(2,1)S(1)} %pad_maximum_fusion, f32[128]{0:T(128)S(1)} %get-tuple-element.135, f32[128]{0:T(128)S(1)} %get-tuple-element.136, f32[128]{0:T(128)S(1)} %get-tuple-element.137, f32[128]{0:T(128)S(1)} %get-tuple-element.138, ...), kind=kLoop, calls=%fused_computation.18 | loop fusion | flops 14622720 | bytes 10330624 | tf_op jit(solution)/shard_map/convert_element_type | solution.py:73
  13.9 43.2 %collective-permute-start.2 = (bf16[2,2,128,560]{2,3,1,0:T(8,128)(2,1)S(1)}, bf16[2,2,128,560]{2,3,1,0:T(8,128)(2,1)S(1)}, u32[]{:S(2)}, u32[]{:S(2)}) collective-permute-start(bf16[2,2,128,560]{2,3,1,0:T(8,128)(2,1)S(1)} %add_convert_fusion), channel_id=1, source_target_pairs={{0,8},{8,0},{16,24},{24,16},{32,40},{40,32},{48,56},{56,48},{64,72... | collective-permute-start | bytes 1720328 | tf_op jit(solution)/shard_map/ppermute | solution.py:38
  57.1 1.2 fusion.45
  58.3 0.3 collective-permute-done.2
  58.7 2.6 %select_bitcast_fusion.1 = (bf16[2,2,128,560,1]{2,3,1,0,4:T(8,128)(2,1)S(1)}, bf16[2,2,128,560,1]{2,3,1,0,4:T(8,128)(2,1)S(1)}) fusion(bf16[2,2,128,560]{2,3,1,0:T(8,128)(2,1)S(1)} %collective-permute-done.2, pred[]{:T(512)S(6)} %eq.153, bf16[2,2,128,576]{2,3,1,0:T(8,128)(2,1)S(1)} %pad_maximum_fusion, f32[128]{0:T(128)S(1)} %get-tuple-element.135, ...), kind=kLoop, calls=%fused_computation.34 | loop fusion | flops 15196160 | bytes 11477505 | tf_op jit(solution)/shard_map/jit(_where)/select_n | solution.py:117
  61.3 0.3 convolution_bitcast_fusion
  61.6 0.3 fusion.1
  62.0 0.2 multiply_subtract_fusion
  62.2 0.2 fusion.8
  62.4 2.4 %add_convert_fusion.1 = bf16[2,2,128,544]{2,3,0,1:T(8,128)(2,1)S(1)} fusion(bf16[2,2,128,560]{2,3,0,1:T(8,128)(2,1)S(1)} %fusion.8, f32[128]{0:T(128)S(1)} %get-tuple-element.118, f32[128]{0:T(128)S(1)} %get-tuple-element.119, f32[128]{0:T(128)S(1)} %get-tuple-element.120, f32[128]{0:T(128)S(1)} %get-tuple-element.121, f32[128]{0:T(128)S(1)} %get-tuple-element.122, ...), kind=kLoop, calls=%fused_computation.21 | loop fusion | flops 14204928 | bytes 10035712 | tf_op jit(solution)/shard_map/convert_element_type | solution.py:73
  64.8 2.1 %collective-permute-start.3 = (bf16[2,2,128,544]{2,3,0,1:T(8,128)(2,1)S(1)}, bf16[2,2,128,544]{2,3,0,1:T(8,128)(2,1)S(1)}, u32[]{:S(2)}, u32[]{:S(2)}) collective-permute-start(bf16[2,2,128,544]{2,3,0,1:T(8,128)(2,1)S(1)} %add_convert_fusion.1), channel_id=1, source_target_pairs={{0,16},{8,24},{16,0},{24,8},{32,48},{40,56},{48,32},{56,40},{64,80... | collective-permute-start | bytes 1671176 | tf_op jit(solution)/shard_map/ppermute | solution.py:38
  66.9 1.2 fusion.47
  68.1 12.4 %collective-permute-done.3 = bf16[2,2,128,544]{2,3,0,1:T(8,128)(2,1)S(1)} collective-permute-done((bf16[2,2,128,544]{2,3,0,1:T(8,128)(2,1)S(1)}, bf16[2,2,128,544]{2,3,0,1:T(8,128)(2,1)S(1)}, u32[]{:S(2)}, u32[]{:S(2)}) %collective-permute-start.3) | collective-permute-done | bytes 557088 | tf_op jit(solution)/shard_map/ppermute | solution.py:38
  80.5 0.4 convolution_bitcast_fusion.2
  80.9 0.4 fusion.3
  81.2 0.1 multiply_subtract_fusion.1
  81.4 0.2 fusion.9
  81.6 2.3 %add_convert_fusion.2 = bf16[2,2,128,528]{2,3,0,1:T(8,128)(2,1)S(1)} fusion(bf16[2,2,128,544]{2,3,0,1:T(8,128)(2,1)S(1)} %fusion.9, f32[128]{0:T(128)S(1)} %get-tuple-element.101, f32[128]{0:T(128)S(1)} %get-tuple-element.102, f32[128]{0:T(128)S(1)} %get-tuple-element.103, f32[128]{0:T(128)S(1)} %get-tuple-element.104, f32[128]{0:T(128)S(1)} %get-tuple-element.105, ...), kind=kLoop, calls=%fused_computation.24 | loop fusion | flops 13787136 | bytes 9740800 | tf_op jit(solution)/shard_map/convert_element_type | solution.py:73
  83.9 2.0 %collective-permute-start.4 = (bf16[2,2,128,528]{2,3,0,1:T(8,128)(2,1)S(1)}, bf16[2,2,128,528]{2,3,0,1:T(8,128)(2,1)S(1)}, u32[]{:S(2)}, u32[]{:S(2)}) collective-permute-start(bf16[2,2,128,528]{2,3,0,1:T(8,128)(2,1)S(1)} %add_convert_fusion.2), channel_id=1, source_target_pairs={{0,32},{8,40},{16,48},{24,56},{32,0},{40,8},{48,16},{56,24},{64,96... | collective-permute-start | bytes 1622024 | tf_op jit(solution)/shard_map/ppermute | solution.py:38
  85.9 1.1 fusion.49
  87.1 25.5 %collective-permute-done.4 = bf16[2,2,128,528]{2,3,0,1:T(8,128)(2,1)S(1)} collective-permute-done((bf16[2,2,128,528]{2,3,0,1:T(8,128)(2,1)S(1)}, bf16[2,2,128,528]{2,3,0,1:T(8,128)(2,1)S(1)}, u32[]{:S(2)}, u32[]{:S(2)}) %collective-permute-start.4) | collective-permute-done | bytes 540704 | tf_op jit(solution)/shard_map/ppermute | solution.py:38
  112.5 0.4 convolution_bitcast_fusion.4
  112.9 0.4 fusion.5
  113.2 0.1 multiply_subtract_fusion.2
  113.4 0.2 fusion.10
  113.6 2.3 %add_convert_fusion.3 = bf16[2,2,128,512]{2,3,0,1:T(8,128)(2,1)S(1)} fusion(bf16[2,2,128,528]{2,3,0,1:T(8,128)(2,1)S(1)} %fusion.10, f32[128]{0:T(128)S(1)} %get-tuple-element.84, f32[128]{0:T(128)S(1)} %get-tuple-element.85, f32[128]{0:T(128)S(1)} %get-tuple-element.86, f32[128]{0:T(128)S(1)} %get-tuple-element.87, f32[128]{0:T(128)S(1)} %get-tuple-element.88, ...), kind=kLoop, calls=%fused_computation.27 | loop fusion | flops 13369344 | bytes 9445888 | tf_op jit(solution)/shard_map/convert_element_type | solution.py:73
  115.9 2.0 %collective-permute-start.5 = (bf16[2,2,128,512]{2,3,0,1:T(8,128)(2,1)S(1)}, bf16[2,2,128,512]{2,3,0,1:T(8,128)(2,1)S(1)}, u32[]{:S(2)}, u32[]{:S(2)}) collective-permute-start(bf16[2,2,128,512]{2,3,0,1:T(8,128)(2,1)S(1)} %add_convert_fusion.3), channel_id=1, source_target_pairs={{0,64},{8,72},{16,80},{24,88},{32,96},{40,104},{48,112},{56,120},{... | collective-permute-start | bytes 1572872 | tf_op jit(solution)/shard_map/ppermute | solution.py:38
  117.9 1.1 fusion.51
  119.0 46.3 %collective-permute-done.5 = bf16[2,2,128,512]{2,3,0,1:T(8,128)(2,1)S(1)} collective-permute-done((bf16[2,2,128,512]{2,3,0,1:T(8,128)(2,1)S(1)}, bf16[2,2,128,512]{2,3,0,1:T(8,128)(2,1)S(1)}, u32[]{:S(2)}, u32[]{:S(2)}) %collective-permute-start.5) | collective-permute-done | bytes 524320 | tf_op jit(solution)/shard_map/ppermute | solution.py:38
  165.3 0.3 convolution_bitcast_fusion.6
  165.7 0.4 fusion.7
  166.0 0.1 multiply_subtract_fusion.3
  166.2 0.2 fusion.11
  166.3 1.0 copy.13
  (37 shorter events, 0.5 us)
Async XLA Ops:
  0.0 7.5 %copy-start = (bf16[4,2,2,2,128,128]{5,4,3,2,1,0:T(8,128)(2,1)S(1)}, bf16[4,2,2,2,128,128]{5,4,3,2,1,0:T(8,128)(2,1)}, u32[]{:S(2)}) copy-start(bf16[4,2,2,2,128,128]{5,4,3,2,1,0:T(8,128)(2,1)} %param.5) | copy-start | bytes 3145732
  1.4 9.9 %collective-permute-start.1 = (bf16[2,2,128,32]{2,3,1,0:T(8,128)(2,1)S(1)}, bf16[2,2,128,32]{2,3,1,0:T(8,128)(2,1)S(1)}, u32[]{:S(2)}, u32[]{:S(2)}) collective-permute-start(bf16[2,2,128,32]{2,3,1,0:T(8,128)(2,1)S(1)} %get-tuple-element.50), channel_id=1, source_target_pairs={{1,0},{2,1},{3,2},{4,3},{5,4},{6,5},{7,6},{9,8},{10,9},{11,10},{12... | collective-permute-start | bytes 98312 | tf_op jit(solution)/shard_map/ppermute | solution.py:28
  2.7 8.6 %collective-permute-start = (bf16[2,2,128,32]{2,3,1,0:T(8,128)(2,1)S(1)}, bf16[2,2,128,32]{2,3,1,0:T(8,128)(2,1)S(1)}, u32[]{:S(2)}, u32[]{:S(2)}) collective-permute-start(bf16[2,2,128,32]{2,3,1,0:T(8,128)(2,1)S(1)} %get-tuple-element.49), channel_id=1, source_target_pairs={{0,1},{1,2},{2,3},{3,4},{4,5},{5,6},{6,7},{8,9},{9,10},{10,11},{11... | collective-permute-start | bytes 98312 | tf_op jit(solution)/shard_map/ppermute | solution.py:26
  7.5 0.7 copy-start.2
  7.7 0.7 copy-start.1
  13.9 44.8 %collective-permute-start.2 = (bf16[2,2,128,560]{2,3,1,0:T(8,128)(2,1)S(1)}, bf16[2,2,128,560]{2,3,1,0:T(8,128)(2,1)S(1)}, u32[]{:S(2)}, u32[]{:S(2)}) collective-permute-start(bf16[2,2,128,560]{2,3,1,0:T(8,128)(2,1)S(1)} %add_convert_fusion), channel_id=1, source_target_pairs={{0,8},{8,0},{16,24},{24,16},{32,40},{40,32},{48,56},{56,48},{64,72... | collective-permute-start | bytes 1720328 | tf_op jit(solution)/shard_map/ppermute | solution.py:38
  64.8 15.7 %collective-permute-start.3 = (bf16[2,2,128,544]{2,3,0,1:T(8,128)(2,1)S(1)}, bf16[2,2,128,544]{2,3,0,1:T(8,128)(2,1)S(1)}, u32[]{:S(2)}, u32[]{:S(2)}) collective-permute-start(bf16[2,2,128,544]{2,3,0,1:T(8,128)(2,1)S(1)} %add_convert_fusion.1), channel_id=1, source_target_pairs={{0,16},{8,24},{16,0},{24,8},{32,48},{40,56},{48,32},{56,40},{64,80... | collective-permute-start | bytes 1671176 | tf_op jit(solution)/shard_map/ppermute | solution.py:38
  83.9 28.6 %collective-permute-start.4 = (bf16[2,2,128,528]{2,3,0,1:T(8,128)(2,1)S(1)}, bf16[2,2,128,528]{2,3,0,1:T(8,128)(2,1)S(1)}, u32[]{:S(2)}, u32[]{:S(2)}) collective-permute-start(bf16[2,2,128,528]{2,3,0,1:T(8,128)(2,1)S(1)} %add_convert_fusion.2), channel_id=1, source_target_pairs={{0,32},{8,40},{16,48},{24,56},{32,0},{40,8},{48,16},{56,24},{64,96... | collective-permute-start | bytes 1622024 | tf_op jit(solution)/shard_map/ppermute | solution.py:38
  115.9 49.4 %collective-permute-start.5 = (bf16[2,2,128,512]{2,3,0,1:T(8,128)(2,1)S(1)}, bf16[2,2,128,512]{2,3,0,1:T(8,128)(2,1)S(1)}, u32[]{:S(2)}, u32[]{:S(2)}) collective-permute-start(bf16[2,2,128,512]{2,3,0,1:T(8,128)(2,1)S(1)} %add_convert_fusion.3), channel_id=1, source_target_pairs={{0,64},{8,72},{16,80},{24,88},{32,96},{40,104},{48,112},{56,120},{... | collective-permute-start | bytes 1572872 | tf_op jit(solution)/shard_map/ppermute | solution.py:38
where the time goes:
time: 168 us; the launch traced here: 167 us
  waiting for transfers between devices  84.5 us (50%)
  starting transfers between devices  55.3 us (33%)
  other arithmetic  20.5 us (12%)
  local copies, waits for them, and re-layouts  3.54 us (2%)
  matrix products  2.8 us (2%)
    ppermute x4, waiting for transfers between devices, from_partner(): return lax.ppermute(value, axis, pairs)  84.5 us
    ppermute x4, starting transfers between devices, from_partner(): return lax.ppermute(value, axis, pairs)  49.3 us
    convert_element_type x4, other arithmetic, interpolate(): return total.astype(jnp.bfloat16)  9.48 us
    ppermute x1, starting transfers between devices, padded_2(): lax.ppermute(tail, axis, [(i, (i + 1) % count) for i in range(ends)])  4.74 us
    cos x4, other arithmetic, rotate(): cosine = jnp.cos(phase)  4.6 us
  transfers between devices with their start and end apart: 6, of which 4 were waited for; matrix products, arithmetic and copies ran while one was open for 5% of the time, Pallas kernels for 0%

commit v1 on v0

v1 whole, which is shorter than its diff:
```python
import math

import jax
import jax.numpy as jnp
from jax import lax
from jax.experimental import pallas as pl
from jax.experimental.pallas import tpu as pltpu
from jax.sharding import PartitionSpec as P

ANGLES = 128
RIM = 8
TAPS = 4
LEVELS = 4
PERIOD = 64
PHASE_STEP = 2.0 * math.pi / PERIOD

MESH = pl.DeviceIdType.MESH
F32 = jnp.float32
BF16 = jnp.bfloat16

CHUNK1 = ((0, 160), (160, 128))
CHUNK2 = ((0, 144), (144, 128))
CHUNK3 = ((0, 128), (128, 128))
ROWS0 = 112
TABLE = 256


def xor2(a, m):
    return (a % 2 + m % 2) % 2 + 2 * ((a // 2 + m // 2) % 2)


def kernel(
    image_hbm, weights_hbm, taps, shifts, out,
    image, weights, wide, cos_t, sin_t, cos_last, sin_last,
    rows_bf, first, from_core, halo, x1, y1, units, x2, x3, y3, turned,
    load_sem, core_sem, halo_send, halo_recv, in_send, in_recv, pair_send, pair_recv, out_send, out_recv,
):
    sub = lax.axis_index("sub")
    rng = lax.axis_index("rng")
    last_rng = lax.axis_size("rng") - 1
    core = sub % 2
    z = sub // 2
    zl = z % 8
    base = z - zl
    quad = zl % 4
    upper = zl // 4
    half = (zl // 2) % 2
    side0 = zl % 2
    width = image.shape[3]
    hw = width // 2

    def device(z_local, core_index):
        return {"sub": (base + z_local) * 2 + core_index}

    partner = {"sub": z * 2 + (1 - core)}
    in_peers = [device(4 * core + xor2(quad, m), upper) for m in range(4)]
    self_in = upper == core
    out_dests = [device(4 * core + xor2(quad, m), side0) for m in range(4)]
    out_sources = [device(2 * k + core, upper) for k in range(4)]
    self_out = jnp.logical_and(upper == core, side0 == core)

    barrier = pltpu.get_barrier_semaphore()

    def greet(who):
        pl.semaphore_signal(barrier, inc=1, device_id=who, device_id_type=MESH)

    greet(partner)
    for c in range(2):
        @pl.when(rng > 0)
        def _():
            greet({"sub": z * 2 + c, "rng": rng - 1})

        @pl.when(rng < last_rng)
        def _():
            greet({"sub": z * 2 + c, "rng": rng + 1})

    for m in range(4):
        if m == 0:
            @pl.when(jnp.logical_not(self_in))
            def _():
                greet(in_peers[0])

            @pl.when(jnp.logical_not(self_out))
            def _():
                greet(out_dests[0])
        else:
            greet(in_peers[m])
            greet(out_dests[m])
    for k in range(4):
        @pl.when(jnp.logical_not(jnp.logical_and(self_out, zl // 2 == k)))
        def _():
            greet(out_sources[k])

    load_image = pltpu.make_async_copy(image_hbm, image, load_sem.at[0])
    load_weights = pltpu.make_async_copy(weights_hbm, weights, load_sem.at[1])
    load_image.start()
    load_weights.start()

    def fill_table(level):
        r = lax.broadcasted_iota(jnp.int32, (PERIOD, ANGLES), 0)
        a = lax.broadcasted_iota(jnp.int32, (PERIOD, ANGLES), 1)
        for h in range(2):
            phase = ((r * (h * ANGLES + a + 1) * (7 + level)) % PERIOD).astype(F32) * PHASE_STEP
            c, s = jnp.cos(phase), jnp.sin(phase)
            for i in range(TABLE // PERIOD):
                cos_t[level, h, pl.ds(i * PERIOD, PERIOD), :] = c
                sin_t[level, h, pl.ds(i * PERIOD, PERIOD), :] = s

    fill_table(0)
    load_image.wait()

    for ch in range(2):
        for j in range(2):
            for k in range(width // 128):
                block = image[ch, j, :, pl.ds(k * 128, 128)].astype(F32).T
                rows_bf[j, ch, pl.ds(k * 128, 128), :] = block.astype(BF16)

    load_weights.wait()

    def fill_wide(level):
        for side in range(2):
            for h in range(2):
                wr = weights[level, side, h, 0].astype(F32).T.astype(BF16)
                wi = weights[level, side, h, 1].astype(F32).T.astype(BF16)
                for c, x, value in ((0, 0, wr), (1, 0, -wi), (0, 1, wi), (1, 1, wr)):
                    wide[level, pl.ds((side * 2 + c) * 128, 128), pl.ds((h * 2 + x) * 128, 128)] = value

    fill_wide(0)

    count = (
        1
        + 2 * jnp.where(rng > 0, 1, 0)
        + 2 * jnp.where(rng < last_rng, 1, 0)
        + jnp.where(self_in, 3, 4)
        + jnp.where(self_out, 6, 8)
    )
    pl.semaphore_wait(barrier, count)

    to_core = pltpu.make_async_remote_copy(
        src_ref=rows_bf.at[1 - core],
        dst_ref=from_core,
        send_sem=core_sem.at[0],
        recv_sem=core_sem.at[1],
        device_id=partner,
        device_id_type=MESH,
    )
    margin = LEVELS * RIM

    def halo_copy(j, lr):
        start = 0 if lr == 0 else width - margin
        return pltpu.make_async_remote_copy(
            src_ref=rows_bf.at[j, :, pl.ds(start, margin), :],
            dst_ref=halo.at[core, lr],
            send_sem=halo_send.at[j, lr],
            recv_sem=halo_recv.at[core, lr],
            device_id={"sub": z * 2 + j, "rng": rng - 1 + 2 * lr},
            device_id_type=MESH,
        )

    def halo_wait(side, lr):
        return pltpu.make_async_remote_copy(
            src_ref=rows_bf.at[0, :, pl.ds(0, margin), :],
            dst_ref=halo.at[side, lr],
            send_sem=halo_send.at[0, lr],
            recv_sem=halo_recv.at[side, lr],
            device_id=partner,
            device_id_type=MESH,
        )

    to_core.start()
    for j in range(2):
        @pl.when(rng > 0)
        def _():
            halo_copy(j, 0).start()

        @pl.when(rng < last_rng)
        def _():
            halo_copy(j, 1).start()

    for ch in range(2):
        first[core, ch, pl.ds(margin, width), :] = rows_bf[core, ch].astype(F32)
    to_core.wait_recv()
    for ch in range(2):
        first[1 - core, ch, pl.ds(margin, width), :] = from_core[ch].astype(F32)

    for lr, start, there in ((1, 0, rng > 0), (0, margin + width, rng < last_rng)):
        @pl.when(there)
        def _():
            for side in range(2):
                halo_wait(side, lr).wait_recv()
                for ch in range(2):
                    first[side, ch, pl.ds(start, margin), :] = halo[side, lr, ch].astype(F32)

        @pl.when(jnp.logical_not(there))
        def _():
            first[:, :, pl.ds(start, margin), :] = jnp.zeros((2, 2, margin, ANGLES), F32)

    def bits_of(row):
        code = row + RIM
        return [((code // v) % 2) == 1 for v in (1, 2, 4, 8)]

    def shift_row(level, side):
        return shifts[level, pl.ds(side, 1), :]

    def interpolate(load, rows, bits, level):
        n = rows + 8
        b0, b1, b2, b3 = bits
        v = jnp.where(
            b3,
            jnp.where(b2, load(12, n), load(8, n)),
            jnp.where(b2, load(4, n), load(0, n)),
        )
        v = jnp.where(b0, pltpu.roll(v, n - 1, 0), v)
        v = jnp.where(b1, pltpu.roll(v, n - 2, 0), v)
        total = v * taps[level, 0]
        for t in range(1, TAPS):
            total = total + pltpu.roll(v, n - t, 0) * taps[level, t]
        return total[:rows].astype(BF16)

    def turn(level, h, start, rows, re, im):
        c = cos_t[level, h, pl.ds(start, rows), :]
        s = sin_t[level, h, pl.ds(start, rows), :]
        return re * c - im * s, re * s + im * c

    bits0 = [bits_of(shift_row(0, side)) for side in range(2)]
    rows1 = width + 2 * (margin - RIM)

    def level0(i, carry):
        b = pl.multiple_of(i * ROWS0, 16)
        parts = []
        for side in range(2):
            for ch in range(2):
                parts.append(interpolate(lambda o, n: first[side, ch, pl.ds(b + o, n), :], ROWS0, bits0[side], 0))
        z = jnp.dot(jnp.concatenate(parts, axis=1), wide[0], preferred_element_type=F32)
        start = pl.multiple_of((b + PERIOD - (margin - RIM)) % PERIOD, 8)
        for h in range(2):
            re, im = turn(0, h, start, ROWS0, z[:, h * 256 : h * 256 + 128], z[:, h * 256 + 128 : h * 256 + 256])
            x1[h, 0, pl.ds(b, ROWS0), :] = re
            x1[h, 1, pl.ds(b, ROWS0), :] = im
        return carry

    lax.fori_loop(0, rows1 // ROWS0, level0, 0)

    @pl.when(rng == 0)
    def _():
        x1[:, :, pl.ds(0, margin - RIM), :] = jnp.zeros((2, 2, margin - RIM, ANGLES), F32)

    @pl.when(rng == last_rng)
    def _():
        x1[:, :, pl.ds(rows1 - (margin - RIM), margin - RIM), :] = jnp.zeros((2, 2, margin - RIM, ANGLES), F32)

    own_bits1 = [((shift_row(1, side0) + RIM) // v) % 2 == 1 for v in (1, 2, 4, 8)]

    def in_copy(m, k):
        start, rows = CHUNK1[k]
        dest = xor2(quad, m)
        src_row = pl.multiple_of((dest // 2) * hw + start, 32)
        return (
            y1.at[dest % 2, :, pl.ds(src_row, rows), :],
            units.at[quad, :, pl.ds(start, rows), :],
            in_send.at[m, k],
            in_recv.at[quad, k],
            in_peers[m],
        )

    def start_copy(parts, local):
        src, dst, send, recv, peer = parts

        def remote():
            pltpu.make_async_remote_copy(
                src_ref=src, dst_ref=dst, send_sem=send, recv_sem=recv, device_id=peer, device_id_type=MESH
            ).start()

        if local is None:
            remote()
        else:
            @pl.when(local)
            def _():
                pltpu.make_async_copy(src, dst, recv).start()

            @pl.when(jnp.logical_not(local))
            def _():
                remote()

    def wait_sent(parts, local):
        src, dst, send, recv, peer = parts

        def wait():
            pltpu.make_async_remote_copy(
                src_ref=src, dst_ref=dst, send_sem=send, recv_sem=recv, device_id=peer, device_id_type=MESH
            ).wait_send()

        if local is None:
            wait()
        else:
            @pl.when(jnp.logical_not(local))
            def _():
                wait()

    for k in range(2):
        start, rows = CHUNK1[k]
        for part in range(2):
            if k == 1 and part == 0:
                rows = hw - start
            else:
                rows = CHUNK1[k][1]
            for h in range(2):
                for ch in range(2):
                    at = part * hw + start
                    y1[h, ch, pl.ds(at, rows), :] = interpolate(
                        lambda o, n: x1[h, ch, pl.ds(at + o, n), :], rows, own_bits1, 1
                    )
        for m in range(4):
            start_copy(in_copy(m, k), self_in if m == 0 else None)

    fill_wide(1)
    fill_table(1)
    fill_wide(2)
    fill_table(2)
    for side in range(2):
        wr = weights[3, side, core, 0]
        wi = weights[3, side, core, 1]
        for c, x, value in ((0, 0, wr), (1, 0, -wi), (0, 1, wi), (1, 1, wr)):
            wide[3, pl.ds(x * 128, 128), pl.ds((side * 2 + c) * 128, 128)] = value
    a = lax.broadcasted_iota(jnp.int32, (ANGLES, 128), 0)
    r = lax.broadcasted_iota(jnp.int32, (ANGLES, 128), 1)
    phase = ((r * (core * ANGLES + a + 1) * (7 + 3)) % PERIOD).astype(F32) * PHASE_STEP
    cos_last[...] = jnp.cos(phase)
    sin_last[...] = jnp.sin(phase)

    bits2 = [bits_of(shift_row(2, side)) for side in range(2)]
    bits3 = bits_of(shift_row(3, core))
    at_start = jnp.logical_and(rng == 0, half == 0)
    at_end = jnp.logical_and(rng == last_rng, half == 1)

    def merge(level, lhs, start_row, rows, margin_rows, dst, slots):
        z = jnp.dot(lhs, wide[level], preferred_element_type=F32)
        start = (start_row - margin_rows) % PERIOD
        for h in range(2):
            re, im = turn(level, h, start, rows, z[:, h * 256 : h * 256 + 128], z[:, h * 256 + 128 : h * 256 + 256])
            dst[slots[h], 0, pl.ds(start_row, rows), :] = re
            dst[slots[h], 1, pl.ds(start_row, rows), :] = im

    def clear(dst, k, margin_rows):
        total = hw + 2 * margin_rows

        @pl.when(at_start if k == 0 else at_end)
        def _():
            at = 0 if k == 0 else total - margin_rows
            dst[:, :, pl.ds(at, margin_rows), :] = jnp.zeros((4, 2, margin_rows, ANGLES), F32)

    def pair_copy(k):
        start, rows = CHUNK3[k]
        ref = y3.at[core, :, :, pl.ds(start, rows), :]
        return pltpu.make_async_remote_copy(
            src_ref=ref, dst_ref=ref, send_sem=pair_send.at[k], recv_sem=pair_recv.at[k],
            device_id=partner, device_id_type=MESH,
        )

    def pair_wait(k):
        start, rows = CHUNK3[k]
        ref = y3.at[1 - core, :, :, pl.ds(start, rows), :]
        return pltpu.make_async_remote_copy(
            src_ref=ref, dst_ref=ref, send_sem=pair_send.at[k], recv_sem=pair_recv.at[k],
            device_id=partner, device_id_type=MESH,
        )

    def out_copy(m, k):
        start, rows = CHUNK3[k]
        dest = xor2(quad, m)
        col = pl.multiple_of(half * hw + start, 128)
        return (
            turned.at[dest, :, :, pl.ds(start, rows)],
            out.at[:, upper, :, pl.ds(col, rows)],
            out_send.at[m, k],
            out_recv.at[zl // 2, k],
            out_dests[m],
        )

    for k in range(2):
        start, rows = CHUNK1[k]
        for s in range(4):
            ref = units.at[s, :, pl.ds(start, rows), :]
            pltpu.make_async_remote_copy(
                src_ref=ref, dst_ref=ref, send_sem=in_send.at[0, k], recv_sem=in_recv.at[s, k],
                device_id=partner, device_id_type=MESH,
            ).wait_recv()
        for p in range(2):
            lhs = jnp.concatenate(
                [units[2 * p + side, ch, pl.ds(start, rows), :] for side in range(2) for ch in range(2)], axis=1
            )
            merge(1, lhs, start, rows, 2 * RIM, x2, (2 * p, 2 * p + 1))
        clear(x2, k, 2 * RIM)
        start, rows = CHUNK2[k]
        for p in range(2):
            lhs = jnp.concatenate(
                [
                    interpolate(lambda o, n: x2[p + 2 * side, ch, pl.ds(start + o, n), :], rows, bits2[side], 2)
                    for side in range(2)
                    for ch in range(2)
                ],
                axis=1,
            )
            merge(2, lhs, start, rows, RIM, x3, (p, p + 2))
        clear(x3, k, RIM)
        start, rows = CHUNK3[k]
        for s in range(4):
            for ch in range(2):
                y3[core, s, ch, pl.ds(start, rows), :] = interpolate(
                    lambda o, n: x3[s, ch, pl.ds(start + o, n), :], rows, bits3, 3
                )
        pair_copy(k).start()
        pair_wait(k).wait_recv()
        for s in range(4):
            rhs = jnp.concatenate(
                [y3[side, s, ch, pl.ds(start, rows), :] for side in range(2) for ch in range(2)], axis=1
            )
            z = lax.dot_general(
                wide[3, pl.ds(0, 256), :], rhs, (((1,), (1,)), ((), ())), preferred_element_type=F32
            )
            re, im = z[:128], z[128:]
            turned[s, 0, :, pl.ds(start, rows)] = (re * cos_last[...] - im * sin_last[...]).astype(BF16)
            turned[s, 1, :, pl.ds(start, rows)] = (re * sin_last[...] + im * cos_last[...]).astype(BF16)
        for m in range(4):
            start_copy(out_copy(m, k), self_out if m == 0 else None)

    to_core.wait_send()
    for j in range(2):
        @pl.when(rng > 0)
        def _():
            halo_copy(j, 0).wait_send()

        @pl.when(rng < last_rng)
        def _():
            halo_copy(j, 1).wait_send()

    for k in range(2):
        for m in range(4):
            wait_sent(in_copy(m, k), self_in if m == 0 else None)
        pair_copy(k).wait_send()
        for m in range(4):
            wait_sent(out_copy(m, k), self_out if m == 0 else None)
    for k in range(2):
        start, rows = CHUNK3[k]
        for s in range(4):
            pltpu.make_async_remote_copy(
                src_ref=turned.at[0, :, :, pl.ds(start, rows)],
                dst_ref=out.at[:, s // 2, :, pl.ds((s % 2) * hw + start, rows)],
                send_sem=out_send.at[0, k],
                recv_sem=out_recv.at[s, k],
                device_id=partner,
                device_id_type=MESH,
            ).wait_recv()


def on_device(image, interp_weights, range_taps, range_shifts):
    width = image.shape[3]
    hw = width // 2
    margin = LEVELS * RIM
    dma = pltpu.SemaphoreType.DMA
    vmem = pltpu.VMEM
    return pl.pallas_call(
        kernel,
        out_shape=jax.ShapeDtypeStruct(image.shape, image.dtype),
        in_specs=[
            pl.BlockSpec(memory_space=pl.ANY),
            pl.BlockSpec(memory_space=pl.ANY),
            pl.BlockSpec(memory_space=pltpu.SMEM),
            pl.BlockSpec(memory_space=pltpu.VMEM),
        ],
        out_specs=pl.BlockSpec(memory_space=pl.ANY),
        scratch_shapes=[
            vmem(image.shape, BF16),
            vmem(interp_weights.shape, BF16),
            vmem((LEVELS, 512, 512), BF16),
            vmem((3, 2, TABLE, ANGLES), F32),
            vmem((3, 2, TABLE, ANGLES), F32),
            vmem((ANGLES, 128), F32),
            vmem((ANGLES, 128), F32),
            vmem((2, 2, width, ANGLES), BF16),
            vmem((2, 2, width + 2 * margin + 16, ANGLES), F32),
            vmem((2, width, ANGLES), BF16),
            vmem((2, 2, 2, margin, ANGLES), BF16),
            vmem((2, 2, width + 6 * RIM + 16, ANGLES), F32),
            vmem((2, 2, width + 4 * RIM, ANGLES), BF16),
            vmem((4, 2, hw + 4 * RIM, ANGLES), BF16),
            vmem((4, 2, hw + 4 * RIM + 16, ANGLES), F32),
            vmem((4, 2, hw + 2 * RIM + 16, ANGLES), F32),
            vmem((2, 4, 2, hw, ANGLES), BF16),
            vmem((4, 2, ANGLES, hw), BF16),
            dma((2,)),
            dma((2,)),
            dma((2, 2)),
            dma((2, 2)),
            dma((4, 2)),
            dma((4, 2)),
            dma((2,)),
            dma((2,)),
            dma((4, 2)),
            dma((4, 2)),
        ],
        compiler_params=pltpu.CompilerParams(collective_id=0, has_side_effects=True),
        name="backprojection",
    )(image, interp_weights, range_taps, range_shifts)


def solution(mesh):
    return jax.shard_map(
        on_device,
        mesh=mesh,
        in_specs=(P(None, ("img", "sub"), None, "rng"), P(), P(), P()),
        out_specs=P(None, ("img", "sub"), None, "rng"),
        check_vma=False,
    )
```

time: 168 us -> 109 us (0.65)
  Pallas kernels: 0 us -> 107 us
  waiting for transfers between devices: 84.5 us -> 0 us
  starting transfers between devices: 55.3 us -> 0 us
  other arithmetic: 20.5 us -> 0 us
  matrix products: 2.8 us -> 0 us
    pallas_call x0 -> x1, Pallas kernels: none -> 107 us  [on_device(): pl.pallas_call(kernel, out_shape=jax.ShapeDtypeStruct(image.shape, image....]
    ppermute x6 -> x0, waiting for transfers between devices: 84.5 us -> none  [the longest x4 84.5 us: from_partner(): return lax.ppermute(value, axis, pairs)]
    ppermute x6 -> x0, starting transfers between devices: 55.3 us -> none  [the longest x4 49.3 us: from_partner(): return lax.ppermute(value, axis, pairs)]
    convert_element_type x8 -> x0, other arithmetic: 10.2 us -> none  [the longest x4 9.48 us: interpolate(): return total.astype(jnp.bfloat16)]
    cos x4 -> x0, other arithmetic: 4.6 us -> none  [rotate(): cosine = jnp.cos(phase)]
    dot_general x8 -> x0, matrix products: 2.8 us -> none  [combine_sides(): jnp.einsum('xcij,cgjr->xgir', block_of(chosen[side_index]), source, prefe...]
    select_n x5 -> x0, other arithmetic: 2.62 us -> none  [the longest x1 2.59 us: on_device(): lower_rows = jnp.where(own_half == 0, own_rows, partner)]
    unnamed x1 -> x0, other arithmetic: 1.71 us -> none
  transfers between devices with their start and end apart: 6 -> 0, of which waited for: 4 -> 0; matrix products, arithmetic and copies ran while one was open for 5% -> 0% of each run, Pallas kernels for 0% -> 0%
where the time goes in v1:
time: 109 us; the launch traced here: 108 us
  Pallas kernels  107 us (98%)
  local copies, waits for them, and re-layouts  1.87 us (2%)
    pallas_call x1, Pallas kernels, on_device(): pl.pallas_call(kernel, out_shape=jax.ShapeDtypeStruct(image.shape, image....  107 us

profile of v1, /device:TPU:65, one launch (start us, length us, event | category | flops | bytes accessed | tf_op | source)
XLA Modules:
  0.0 108.5 jit_solution(12517677964275607808)
XLA Ops:
  0.0 106.6 %backprojection.1 = bf16[2,2,128,512]{3,2,1,0:T(8,128)(2,1)} custom-call(bf16[2,2,128,512]{3,2,1,0:T(8,128)(2,1)} %image_hbm.1, bf16[4,2,2,2,128,128]{5,4,3,2,1,0:T(8,128)(2,1)} %weights_hbm.1, f32[4,4]{1,0:T(4,128)} %taps.1, s32[4,2,128]{2,1,0:T(2,128)} %shifts.1), custom_call_target="tpu_custom_call" | custom-call | tf_op jit(solution)/shard_map/backprojection/pallas_call | solution.py:462
  106.6 1.9 %copy.6 = bf16[2,2,128,512]{3,2,1,0:T(8,128)(2,1)} copy(bf16[2,2,128,512]{3,2,1,0:T(8,128)(2,1)} %backprojection.1) | data formatting | bytes 1048576

commit v2 on v1

--- a/solution.py
+++ b/solution.py
@@ -21,12 +21,8 @@
 CHUNK1 = ((0, 160), (160, 128))
 CHUNK2 = ((0, 144), (144, 128))
 CHUNK3 = ((0, 128), (128, 128))
-ROWS0 = 112
+ROWS0 = (((0, 176), (256, 176)), ((176, 80), (432, 128)))
 TABLE = 256
-
-
-def xor2(a, m):
-    return (a % 2 + m % 2) % 2 + 2 * ((a // 2 + m // 2) % 2)
 
 
 def kernel(
@@ -34,6 +30,7 @@
     image, weights, wide, cos_t, sin_t, cos_last, sin_last,
     rows_bf, first, from_core, halo, x1, y1, units, x2, x3, y3, turned,
     load_sem, core_sem, halo_send, halo_recv, in_send, in_recv, pair_send, pair_recv, out_send, out_recv,
+    ready_core, ready_rng, ready_in, ready_out,
 ):
     sub = lax.axis_index("sub")
     rng = lax.axis_index("rng")
@@ -49,52 +46,81 @@
     width = image.shape[3]
     hw = width // 2
 
-    def device(z_local, core_index):
-        return {"sub": (base + z_local) * 2 + core_index}
-
-    partner = {"sub": z * 2 + (1 - core)}
-    in_peers = [device(4 * core + xor2(quad, m), upper) for m in range(4)]
-    self_in = upper == core
-    out_dests = [device(4 * core + xor2(quad, m), side0) for m in range(4)]
-    out_sources = [device(2 * k + core, upper) for k in range(4)]
-    self_out = jnp.logical_and(upper == core, side0 == core)
-
-    barrier = pltpu.get_barrier_semaphore()
-
-    def greet(who):
-        pl.semaphore_signal(barrier, inc=1, device_id=who, device_id_type=MESH)
-
-    greet(partner)
-    for c in range(2):
-        @pl.when(rng > 0)
-        def _():
-            greet({"sub": z * 2 + c, "rng": rng - 1})
-
-        @pl.when(rng < last_rng)
-        def _():
-            greet({"sub": z * 2 + c, "rng": rng + 1})
-
-    for m in range(4):
-        if m == 0:
-            @pl.when(jnp.logical_not(self_in))
-            def _():
-                greet(in_peers[0])
-
-            @pl.when(jnp.logical_not(self_out))
-            def _():
-                greet(out_dests[0])
-        else:
-            greet(in_peers[m])
-            greet(out_dests[m])
-    for k in range(4):
-        @pl.when(jnp.logical_not(jnp.logical_and(self_out, zl // 2 == k)))
-        def _():
-            greet(out_sources[k])
-
     load_image = pltpu.make_async_copy(image_hbm, image, load_sem.at[0])
     load_weights = pltpu.make_async_copy(weights_hbm, weights, load_sem.at[1])
     load_image.start()
     load_weights.start()
+
+    def device(z_local, core_index):
+        return {"sub": (base + z_local) * 2 + core_index}
+
+    def order(z_local, core_index):
+        return ((z_local + 7) % 8) * 2 + (1 - core_index)
+
+    me = order(zl, core)
+    partner = {"sub": z * 2 + (1 - core)}
+    in_chips = [4 * core + q for q in range(4)]
+    in_self = [jnp.logical_and(upper == core, quad == q) for q in range(4)]
+    in_peers = [device(chip, upper) for chip in in_chips]
+    in_later = [order(chip, upper) > me for chip in in_chips]
+    out_self = [jnp.logical_and(in_self[q], side0 == core) for q in range(4)]
+    out_dests = [device(chip, side0) for chip in in_chips]
+    out_later = [order(chip, side0) > me for chip in in_chips]
+    source_chips = [2 * k + core for k in range(4)]
+    source_self = [jnp.logical_and(zl == source_chips[k], upper == core) for k in range(4)]
+    out_sources = [device(chip, upper) for chip in source_chips]
+    source_later = [order(chip, upper) > me for chip in source_chips]
+    lower_rng, upper_rng = rng > 0, rng < last_rng
+
+    barrier = pltpu.get_barrier_semaphore()
+
+    def greet(who):
+        pl.semaphore_signal(barrier, inc=1, device_id=who, device_id_type=MESH)
+
+    def answer(sem, who):
+        pl.semaphore_signal(sem, inc=1, device_id=who, device_id_type=MESH)
+
+    def earlier(later, own):
+        return jnp.logical_not(jnp.logical_or(later, own))
+
+    @pl.when(core == 1)
+    def _():
+        greet(partner)
+
+    @pl.when(lower_rng)
+    def _():
+        for c in range(2):
+            greet({"sub": z * 2 + c, "rng": rng - 1})
+
+    for peers, later in ((in_peers, in_later), (out_dests, out_later), (out_sources, source_later)):
+        for q in range(4):
+            @pl.when(later[q])
+            def _():
+                greet(peers[q])
+
+    count = jnp.where(core == 0, 1, 0) + jnp.where(upper_rng, 2, 0)
+    for later, own in ((in_later, in_self), (out_later, out_self), (source_later, source_self)):
+        for q in range(4):
+            count = count + jnp.where(earlier(later[q], own[q]), 1, 0)
+    pl.when(count > 0)(lambda: pl.semaphore_wait(barrier, count))
+
+    @pl.when(upper_rng)
+    def _():
+        for c in range(2):
+            answer(ready_rng.at[core], {"sub": z * 2 + c, "rng": rng + 1})
+
+    @pl.when(core == 0)
+    def _():
+        answer(ready_core, partner)
+
+    for q in range(4):
+        @pl.when(earlier(in_later[q], in_self[q]))
+        def _():
+            answer(ready_in.at[quad], in_peers[q])
+
+        @pl.when(earlier(source_later[q], source_self[q]))
+        def _():
+            answer(ready_out.at[quad], out_sources[q])
 
     def fill_table(level):
         r = lax.broadcasted_iota(jnp.int32, (PERIOD, ANGLES), 0)
@@ -106,7 +132,6 @@
                 cos_t[level, h, pl.ds(i * PERIOD, PERIOD), :] = c
                 sin_t[level, h, pl.ds(i * PERIOD, PERIOD), :] = s
 
-    fill_table(0)
     load_image.wait()
 
     for ch in range(2):
@@ -114,8 +139,6 @@
             for k in range(width // 128):
                 block = image[ch, j, :, pl.ds(k * 128, 128)].astype(F32).T
                 rows_bf[j, ch, pl.ds(k * 128, 128), :] = block.astype(BF16)
-
-    load_weights.wait()
 
     def fill_wide(level):
         for side in range(2):
@@ -124,17 +147,6 @@
                 wi = weights[level, side, h, 1].astype(F32).T.astype(BF16)
                 for c, x, value in ((0, 0, wr), (1, 0, -wi), (0, 1, wi), (1, 1, wr)):
                     wide[level, pl.ds((side * 2 + c) * 128, 128), pl.ds((h * 2 + x) * 128, 128)] = value
-
-    fill_wide(0)
-
-    count = (
-        1
-        + 2 * jnp.where(rng > 0, 1, 0)
-        + 2 * jnp.where(rng < last_rng, 1, 0)
-        + jnp.where(self_in, 3, 4)
-        + jnp.where(self_out, 6, 8)
-    )
-    pl.semaphore_wait(barrier, count)
 
     to_core = pltpu.make_async_remote_copy(
         src_ref=rows_bf.at[1 - core],
@@ -167,15 +179,26 @@
             device_id_type=MESH,
         )
 
+    @pl.when(core == 1)
+    def _():
+        pl.semaphore_wait(ready_core, 1)
+
     to_core.start()
-    for j in range(2):
-        @pl.when(rng > 0)
-        def _():
+
+    @pl.when(upper_rng)
+    def _():
+        for j in range(2):
+            halo_copy(j, 1).start()
+
+    load_weights.wait()
+    fill_wide(0)
+    fill_table(0)
+
+    @pl.when(lower_rng)
+    def _():
+        for j in range(2):
+            pl.semaphore_wait(ready_rng.at[j], 1)
             halo_copy(j, 0).start()
-
-        @pl.when(rng < last_rng)
-        def _():
-            halo_copy(j, 1).start()
 
     for ch in range(2):
         first[core, ch, pl.ds(margin, width), :] = rows_bf[core, ch].astype(F32)
@@ -183,7 +206,7 @@
     for ch in range(2):
         first[1 - core, ch, pl.ds(margin, width), :] = from_core[ch].astype(F32)
 
-    for lr, start, there in ((1, 0, rng > 0), (0, margin + width, rng < last_rng)):
+    for lr, start, there in ((1, 0, lower_rng), (0, margin + width, upper_rng)):
         @pl.when(there)
         def _():
             for side in range(2):
@@ -225,80 +248,63 @@
     bits0 = [bits_of(shift_row(0, side)) for side in range(2)]
     rows1 = width + 2 * (margin - RIM)
 
-    def level0(i, carry):
-        b = pl.multiple_of(i * ROWS0, 16)
+    def level0(b, rows):
         parts = []
         for side in range(2):
             for ch in range(2):
-                parts.append(interpolate(lambda o, n: first[side, ch, pl.ds(b + o, n), :], ROWS0, bits0[side], 0))
-        z = jnp.dot(jnp.concatenate(parts, axis=1), wide[0], preferred_element_type=F32)
-        start = pl.multiple_of((b + PERIOD - (margin - RIM)) % PERIOD, 8)
+                parts.append(interpolate(lambda o, n: first[side, ch, pl.ds(b + o, n), :], rows, bits0[side], 0))
+        merged = jnp.dot(jnp.concatenate(parts, axis=1), wide[0], preferred_element_type=F32)
+        start = (b - (margin - RIM)) % PERIOD
         for h in range(2):
-            re, im = turn(0, h, start, ROWS0, z[:, h * 256 : h * 256 + 128], z[:, h * 256 + 128 : h * 256 + 256])
-            x1[h, 0, pl.ds(b, ROWS0), :] = re
-            x1[h, 1, pl.ds(b, ROWS0), :] = im
-        return carry
-
-    lax.fori_loop(0, rows1 // ROWS0, level0, 0)
-
-    @pl.when(rng == 0)
-    def _():
-        x1[:, :, pl.ds(0, margin - RIM), :] = jnp.zeros((2, 2, margin - RIM, ANGLES), F32)
-
-    @pl.when(rng == last_rng)
-    def _():
-        x1[:, :, pl.ds(rows1 - (margin - RIM), margin - RIM), :] = jnp.zeros((2, 2, margin - RIM, ANGLES), F32)
+            re, im = merged[:, h * 256 : h * 256 + 128], merged[:, h * 256 + 128 : h * 256 + 256]
+            re, im = turn(0, h, start, rows, re, im)
+            x1[h, 0, pl.ds(b, rows), :] = re
+            x1[h, 1, pl.ds(b, rows), :] = im
+
+    def clear1(start):
+        x1[:, :, pl.ds(start, margin - RIM), :] = jnp.zeros((2, 2, margin - RIM, ANGLES), F32)
 
     own_bits1 = [((shift_row(1, side0) + RIM) // v) % 2 == 1 for v in (1, 2, 4, 8)]
 
-    def in_copy(m, k):
+    def in_copy(q, k):
         start, rows = CHUNK1[k]
-        dest = xor2(quad, m)
-        src_row = pl.multiple_of((dest // 2) * hw + start, 32)
         return (
-            y1.at[dest % 2, :, pl.ds(src_row, rows), :],
+            y1.at[q % 2, :, pl.ds((q // 2) * hw + start, rows), :],
             units.at[quad, :, pl.ds(start, rows), :],
-            in_send.at[m, k],
+            in_send.at[q, k],
             in_recv.at[quad, k],
-            in_peers[m],
+            in_peers[q],
+        )
+
+    def remote(src, dst, send, recv, peer):
+        return pltpu.make_async_remote_copy(
+            src_ref=src, dst_ref=dst, send_sem=send, recv_sem=recv, device_id=peer, device_id_type=MESH
         )
 
     def start_copy(parts, local):
         src, dst, send, recv, peer = parts
 
-        def remote():
-            pltpu.make_async_remote_copy(
-                src_ref=src, dst_ref=dst, send_sem=send, recv_sem=recv, device_id=peer, device_id_type=MESH
-            ).start()
-
-        if local is None:
-            remote()
+        @pl.when(local)
+        def _():
+            pltpu.make_async_copy(src, dst, recv).start()
+
+        @pl.when(jnp.logical_not(local))
+        def _():
+            remote(*parts).start()
+
+    def wait_sent(parts, local):
+        @pl.when(jnp.logical_not(local))
+        def _():
+            remote(*parts).wait_send()
+
+    for k in range(2):
+        for b, rows in ROWS0[k]:
+            level0(b, rows)
+        if k == 0:
+            pl.when(jnp.logical_not(lower_rng))(lambda: clear1(0))
         else:
-            @pl.when(local)
-            def _():
-                pltpu.make_async_copy(src, dst, recv).start()
-
-            @pl.when(jnp.logical_not(local))
-            def _():
-                remote()
-
-    def wait_sent(parts, local):
-        src, dst, send, recv, peer = parts
-
-        def wait():
-            pltpu.make_async_remote_copy(
-                src_ref=src, dst_ref=dst, send_sem=send, recv_sem=recv, device_id=peer, device_id_type=MESH
-            ).wait_send()
-
-        if local is None:
-            wait()
-        else:
-            @pl.when(jnp.logical_not(local))
-            def _():
-                wait()
-
-    for k in range(2):
-        start, rows = CHUNK1[k]
+            pl.when(jnp.logical_not(upper_rng))(lambda: clear1(rows1 - (margin - RIM)))
+        start = CHUNK1[k][0]
         for part in range(2):
             if k == 1 and part == 0:
                 rows = hw - start
@@ -310,8 +316,10 @@
                     y1[h, ch, pl.ds(at, rows), :] = interpolate(
                         lambda o, n: x1[h, ch, pl.ds(at + o, n), :], rows, own_bits1, 1
                     )
-        for m in range(4):
-            start_copy(in_copy(m, k), self_in if m == 0 else None)
+        for q in (3, 2, 1, 0):
+            if k == 0:
+                pl.when(in_later[q])(lambda: pl.semaphore_wait(ready_in.at[q], 1))
+            start_copy(in_copy(q, k), in_self[q])
 
     fill_wide(1)
     fill_table(1)
@@ -365,16 +373,15 @@
             device_id=partner, device_id_type=MESH,
         )
 
-    def out_copy(m, k):
+    def out_copy(q, k):
         start, rows = CHUNK3[k]
-        dest = xor2(quad, m)
         col = pl.multiple_of(half * hw + start, 128)
         return (
-            turned.at[dest, :, :, pl.ds(start, rows)],
+            turned.at[q, :, :, pl.ds(start, rows)],
             out.at[:, upper, :, pl.ds(col, rows)],
-            out_send.at[m, k],
+            out_send.at[q, k],
             out_recv.at[zl // 2, k],
-            out_dests[m],
+            out_dests[q],
         )
 
     for k in range(2):
@@ -421,25 +428,27 @@
             re, im = z[:128], z[128:]
             turned[s, 0, :, pl.ds(start, rows)] = (re * cos_last[...] - im * sin_last[...]).astype(BF16)
             turned[s, 1, :, pl.ds(start, rows)] = (re * sin_last[...] + im * cos_last[...]).astype(BF16)
-        for m in range(4):
-            start_copy(out_copy(m, k), self_out if m == 0 else None)
+        for q in (3, 2, 1, 0):
+            if k == 0:
+                pl.when(out_later[q])(lambda: pl.semaphore_wait(ready_out.at[q], 1))
+            start_copy(out_copy(q, k), out_self[q])
 
     to_core.wait_send()
     for j in range(2):
-        @pl.when(rng > 0)
+        @pl.when(lower_rng)
         def _():
             halo_copy(j, 0).wait_send()
 
-        @pl.when(rng < last_rng)
+        @pl.when(upper_rng)
         def _():
             halo_copy(j, 1).wait_send()
 
     for k in range(2):
-        for m in range(4):
-            wait_sent(in_copy(m, k), self_in if m == 0 else None)
+        for q in range(4):
+            wait_sent(in_copy(q, k), in_self[q])
         pair_copy(k).wait_send()
-        for m in range(4):
-            wait_sent(out_copy(m, k), self_out if m == 0 else None)
+        for q in range(4):
+            wait_sent(out_copy(q, k), out_self[q])
     for k in range(2):
         start, rows = CHUNK3[k]
         for s in range(4):
@@ -498,6 +507,10 @@
             dma((2,)),
             dma((4, 2)),
             dma((4, 2)),
+            pltpu.SemaphoreType.REGULAR,
+            pltpu.SemaphoreType.REGULAR((2,)),
+            pltpu.SemaphoreType.REGULAR((4,)),
+            pltpu.SemaphoreType.REGULAR((4,)),
         ],
         compiler_params=pltpu.CompilerParams(collective_id=0, has_side_effects=True),
         name="backprojection",

time: 109 us -> 85.7 us (0.79)
  Pallas kernels: 107 us -> 83.6 us
    pallas_call x1, Pallas kernels: 107 us -> 83.6 us  [on_device(): pl.pallas_call(kernel, out_shape=jax.ShapeDtypeStruct(image.shape, image....]
where the time goes in v2:
time: 85.7 us; the launch traced here: 85.5 us
  Pallas kernels  83.6 us (98%)
  local copies, waits for them, and re-layouts  1.87 us (2%)
    pallas_call x1, Pallas kernels, on_device(): pl.pallas_call(kernel, out_shape=jax.ShapeDtypeStruct(image.shape, image....  83.6 us
    unnamed x1, local copies, waits for them, and re-layouts  1.87 us

profile of v2, /device:TPU:65, one launch (start us, length us, event | category | flops | bytes accessed | tf_op | source)
XLA Modules:
  0.0 85.5 jit_solution(14077144104793842794)
XLA Ops:
  0.0 83.6 %backprojection.1 = bf16[2,2,128,512]{3,2,1,0:T(8,128)(2,1)} custom-call(bf16[2,2,128,512]{3,2,1,0:T(8,128)(2,1)} %image_hbm.1, bf16[4,2,2,2,128,128]{5,4,3,2,1,0:T(8,128)(2,1)} %weights_hbm.1, f32[4,4]{1,0:T(4,128)} %taps.1, s32[4,2,128]{2,1,0:T(2,128)} %shifts.1), custom_call_target="tpu_custom_call" | custom-call | tf_op jit(solution)/shard_map/backprojection/pallas_call | solution.py:471
  83.6 1.9 %copy.6 = bf16[2,2,128,512]{3,2,1,0:T(8,128)(2,1)} copy(bf16[2,2,128,512]{3,2,1,0:T(8,128)(2,1)} %backprojection.1) | data formatting | bytes 1048576

commit v3 on v2

--- a/solution.py
+++ b/solution.py
@@ -21,13 +21,13 @@
 CHUNK1 = ((0, 160), (160, 128))
 CHUNK2 = ((0, 144), (144, 128))
 CHUNK3 = ((0, 128), (128, 128))
-ROWS0 = (((0, 176), (256, 176)), ((176, 80), (432, 128)))
+ROWS0 = (((256, 176), (0, 176)), ((176, 80), (432, 128)))
 TABLE = 256
 
 
 def kernel(
-    image_hbm, weights_hbm, taps, shifts, out,
-    image, weights, wide, cos_t, sin_t, cos_last, sin_last,
+    image_hbm, weights_hbm, taps_hbm, shifts_hbm, out,
+    image, weights, taps, shifts, wide, cos_t, sin_t, cos_last, sin_last,
     rows_bf, first, from_core, halo, x1, y1, units, x2, x3, y3, turned,
     load_sem, core_sem, halo_send, halo_recv, in_send, in_recv, pair_send, pair_recv, out_send, out_recv,
     ready_core, ready_rng, ready_in, ready_out,
@@ -48,14 +48,18 @@
 
     load_image = pltpu.make_async_copy(image_hbm, image, load_sem.at[0])
     load_weights = pltpu.make_async_copy(weights_hbm, weights, load_sem.at[1])
+    load_taps = pltpu.make_async_copy(taps_hbm, taps, load_sem.at[2])
+    load_shifts = pltpu.make_async_copy(shifts_hbm, shifts, load_sem.at[3])
     load_image.start()
     load_weights.start()
+    load_taps.start()
+    load_shifts.start()
 
     def device(z_local, core_index):
         return {"sub": (base + z_local) * 2 + core_index}
 
     def order(z_local, core_index):
-        return ((z_local + 7) % 8) * 2 + (1 - core_index)
+        return jnp.where(z_local * 2 + core_index == 0, 16, z_local * 2 + (1 - core_index))
 
     me = order(zl, core)
     partner = {"sub": z * 2 + (1 - core)}
@@ -190,6 +194,8 @@
         for j in range(2):
             halo_copy(j, 1).start()
 
+    load_taps.wait()
+    load_shifts.wait()
     load_weights.wait()
     fill_wide(0)
     fill_table(0)
@@ -206,7 +212,9 @@
     for ch in range(2):
         first[1 - core, ch, pl.ds(margin, width), :] = from_core[ch].astype(F32)
 
-    for lr, start, there in ((1, 0, lower_rng), (0, margin + width, upper_rng)):
+    def take_halo(lr):
+        start, there = ((margin + width, upper_rng), (0, lower_rng))[lr]
+
         @pl.when(there)
         def _():
             for side in range(2):
@@ -266,15 +274,29 @@
 
     own_bits1 = [((shift_row(1, side0) + RIM) // v) % 2 == 1 for v in (1, 2, 4, 8)]
 
-    def in_copy(q, k):
+    def nth(i):
+        q = jnp.where(jnp.logical_and(core == 1, zl > 0), i, 3 - i)
+        chip = 4 * core + q
+        own = jnp.logical_and(upper == core, quad == q)
+        return q, own, device(chip, upper), order(chip, upper) > me
+
+    def in_copy(i, k):
         start, rows = CHUNK1[k]
+        q, own, peer, later = nth(i)
+        row = pl.multiple_of((q // 2) * hw + start, 32)
         return (
-            y1.at[q % 2, :, pl.ds((q // 2) * hw + start, rows), :],
+            y1.at[q % 2, :, pl.ds(row, rows), :],
             units.at[quad, :, pl.ds(start, rows), :],
-            in_send.at[q, k],
+            in_send.at[i, k],
             in_recv.at[quad, k],
-            in_peers[q],
-        )
+            peer,
+        )
+
+    def send_unit(i, k):
+        q, own, peer, later = nth(i)
+        if k == 0:
+            pl.when(later)(lambda: pl.semaphore_wait(ready_in.at[q], 1))
+        start_copy(in_copy(i, k), own)
 
     def remote(src, dst, send, recv, peer):
         return pltpu.make_async_remote_copy(
@@ -298,8 +320,9 @@
             remote(*parts).wait_send()
 
     for k in range(2):
-        for b, rows in ROWS0[k]:
-            level0(b, rows)
+        level0(*ROWS0[k][0])
+        take_halo(1 - k)
+        level0(*ROWS0[k][1])
         if k == 0:
             pl.when(jnp.logical_not(lower_rng))(lambda: clear1(0))
         else:
@@ -316,10 +339,13 @@
                     y1[h, ch, pl.ds(at, rows), :] = interpolate(
                         lambda o, n: x1[h, ch, pl.ds(at + o, n), :], rows, own_bits1, 1
                     )
-        for q in (3, 2, 1, 0):
-            if k == 0:
-                pl.when(in_later[q])(lambda: pl.semaphore_wait(ready_in.at[q], 1))
-            start_copy(in_copy(q, k), in_self[q])
+        for i in range(3):
+            send_unit(i, k)
+        if k == 0:
+            pl.when(zl == 0)(lambda: send_unit(3, 0))
+        else:
+            pl.when(zl > 0)(lambda: send_unit(3, 0))
+            send_unit(3, 1)
 
     fill_wide(1)
     fill_table(1)
@@ -373,16 +399,29 @@
             device_id=partner, device_id_type=MESH,
         )
 
-    def out_copy(q, k):
+    def nth_out(i):
+        q = core * (3 - i) + (1 - core) * i
+        chip = 4 * core + q
+        own = jnp.logical_and(jnp.logical_and(upper == core, side0 == core), quad == q)
+        return q, own, device(chip, side0), order(chip, side0) > me
+
+    def out_copy(i, k):
         start, rows = CHUNK3[k]
+        q, own, peer, later = nth_out(i)
         col = pl.multiple_of(half * hw + start, 128)
         return (
             turned.at[q, :, :, pl.ds(start, rows)],
             out.at[:, upper, :, pl.ds(col, rows)],
-            out_send.at[q, k],
+            out_send.at[i, k],
             out_recv.at[zl // 2, k],
-            out_dests[q],
-        )
+            peer,
+        )
+
+    def send_block(i, k):
+        q, own, peer, later = nth_out(i)
+        if k == 0:
+            pl.when(later)(lambda: pl.semaphore_wait(ready_out.at[q], 1))
+        start_copy(out_copy(i, k), own)
 
     for k in range(2):
         start, rows = CHUNK1[k]
@@ -428,10 +467,8 @@
             re, im = z[:128], z[128:]
             turned[s, 0, :, pl.ds(start, rows)] = (re * cos_last[...] - im * sin_last[...]).astype(BF16)
             turned[s, 1, :, pl.ds(start, rows)] = (re * sin_last[...] + im * cos_last[...]).astype(BF16)
-        for q in (3, 2, 1, 0):
-            if k == 0:
-                pl.when(out_later[q])(lambda: pl.semaphore_wait(ready_out.at[q], 1))
-            start_copy(out_copy(q, k), out_self[q])
+        for i in range(4):
+            send_block(i, k)
 
     to_core.wait_send()
     for j in range(2):
@@ -444,11 +481,11 @@
             halo_copy(j, 1).wait_send()
 
     for k in range(2):
-        for q in range(4):
-            wait_sent(in_copy(q, k), in_self[q])
+        for i in range(4):
+            wait_sent(in_copy(i, k), nth(i)[1])
         pair_copy(k).wait_send()
-        for q in range(4):
-            wait_sent(out_copy(q, k), out_self[q])
+        for i in range(4):
+            wait_sent(out_copy(i, k), nth_out(i)[1])
     for k in range(2):
         start, rows = CHUNK3[k]
         for s in range(4):
@@ -470,17 +507,19 @@
     vmem = pltpu.VMEM
     return pl.pallas_call(
         kernel,
-        out_shape=jax.ShapeDtypeStruct(image.shape, image.dtype),
+        out_shape=pltpu.VMEM(image.shape, image.dtype),
         in_specs=[
             pl.BlockSpec(memory_space=pl.ANY),
             pl.BlockSpec(memory_space=pl.ANY),
-            pl.BlockSpec(memory_space=pltpu.SMEM),
-            pl.BlockSpec(memory_space=pltpu.VMEM),
+            pl.BlockSpec(memory_space=pl.ANY),
+            pl.BlockSpec(memory_space=pl.ANY),
         ],
-        out_specs=pl.BlockSpec(memory_space=pl.ANY),
+        out_specs=pl.BlockSpec(memory_space=pltpu.VMEM),
         scratch_shapes=[
             vmem(image.shape, BF16),
             vmem(interp_weights.shape, BF16),
+            pltpu.SMEM(range_taps.shape, F32),
+            vmem(range_shifts.shape, jnp.int32),
             vmem((LEVELS, 512, 512), BF16),
             vmem((3, 2, TABLE, ANGLES), F32),
             vmem((3, 2, TABLE, ANGLES), F32),
@@ -497,7 +536,7 @@
             vmem((4, 2, hw + 2 * RIM + 16, ANGLES), F32),
             vmem((2, 4, 2, hw, ANGLES), BF16),
             vmem((4, 2, ANGLES, hw), BF16),
-            dma((2,)),
+            dma((4,)),
             dma((2,)),
             dma((2, 2)),
             dma((2, 2)),

time: 85.7 us -> 80.7 us (0.942)
  Pallas kernels: 83.6 us -> 79.8 us
  local copies, waits for them, and re-layouts: 1.87 us -> 0.8 us
    pallas_call x1, Pallas kernels: 83.6 us -> 79.8 us  [on_device(): pl.pallas_call(kernel, out_shape=pltpu.VMEM(image.shape, image.dtype), in...]
    unnamed x1, local copies, waits for them, and re-layouts: 1.87 us -> 0.8 us
where the time goes in v3:
time: 80.7 us; the launch traced here: 80.6 us
  Pallas kernels  79.8 us (99%)
    pallas_call x1, Pallas kernels, on_device(): pl.pallas_call(kernel, out_shape=pltpu.VMEM(image.shape, image.dtype), in...  79.8 us

profile of v3, /device:TPU:65, one launch (start us, length us, event | category | flops | bytes accessed | tf_op | source)
XLA Modules:
  0.0 80.6 jit_solution(18383803712250020726)
XLA Ops:
  0.0 79.8 %backprojection.1 = bf16[2,2,128,512]{3,2,1,0:T(8,128)(2,1)S(1)} custom-call(bf16[2,2,128,512]{3,2,1,0:T(8,128)(2,1)} %image_hbm.1, bf16[4,2,2,2,128,128]{5,4,3,2,1,0:T(8,128)(2,1)} %weights_hbm.1, f32[4,4]{1,0:T(4,128)} %taps_hbm.1, s32[4,2,128]{2,1,0:T(2,128)} %shifts_hbm.1), custom_call_target="tpu_custom_call" | custom-call | tf_op jit(solution)/shard_map/backprojection/pallas_call | solution.py:508
  79.8 0.8 copy.6

commit v4 on v3

--- a/solution.py
+++ b/solution.py
@@ -18,17 +18,18 @@
 F32 = jnp.float32
 BF16 = jnp.bfloat16
 
-CHUNK1 = ((0, 160), (160, 128))
-CHUNK2 = ((0, 144), (144, 128))
-CHUNK3 = ((0, 128), (128, 128))
-ROWS0 = (((256, 176), (0, 176)), ((176, 80), (432, 128)))
+CHUNK1 = ((0, 96), (96, 64), (160, 128))
+CHUNK2 = ((0, 80), (80, 64), (144, 128))
+CHUNK3 = ((0, 64), (64, 64), (128, 128))
+CHUNKS = len(CHUNK3)
+ROWS0 = (((256, 112), (0, 112)), ((112, 64), (368, 64)), ((176, 80), (432, 128)))
 TABLE = 256
 
 
 def kernel(
     image_hbm, weights_hbm, taps_hbm, shifts_hbm, out,
-    image, weights, taps, shifts, wide, cos_t, sin_t, cos_last, sin_last,
-    rows_bf, first, from_core, halo, x1, y1, units, x2, x3, y3, turned,
+    image, weights, taps, shifts, wide, cos_t, sin_t,
+    rows_bf, first, from_core, halo, x1, y1, units, x2, x3, y3, turned, blocks,
     load_sem, core_sem, halo_send, halo_recv, in_send, in_recv, pair_send, pair_recv, out_send, out_recv,
     ready_core, ready_rng, ready_in, ready_out,
 ):
@@ -126,15 +127,18 @@
         def _():
             answer(ready_out.at[quad], out_sources[q])
 
-    def fill_table(level):
+    def fill_phase(level, h, place):
         r = lax.broadcasted_iota(jnp.int32, (PERIOD, ANGLES), 0)
         a = lax.broadcasted_iota(jnp.int32, (PERIOD, ANGLES), 1)
+        phase = ((r * (h * ANGLES + a + 1) * (7 + level)) % PERIOD).astype(F32) * PHASE_STEP
+        c, s = jnp.cos(phase), jnp.sin(phase)
+        for i in range(TABLE // PERIOD):
+            cos_t[level, place, pl.ds(i * PERIOD, PERIOD), :] = c
+            sin_t[level, place, pl.ds(i * PERIOD, PERIOD), :] = s
+
+    def fill_table(level):
         for h in range(2):
-            phase = ((r * (h * ANGLES + a + 1) * (7 + level)) % PERIOD).astype(F32) * PHASE_STEP
-            c, s = jnp.cos(phase), jnp.sin(phase)
-            for i in range(TABLE // PERIOD):
-                cos_t[level, h, pl.ds(i * PERIOD, PERIOD), :] = c
-                sin_t[level, h, pl.ds(i * PERIOD, PERIOD), :] = s
+            fill_phase(level, h, h)
 
     load_image.wait()
 
@@ -144,13 +148,16 @@
                 block = image[ch, j, :, pl.ds(k * 128, 128)].astype(F32).T
                 rows_bf[j, ch, pl.ds(k * 128, 128), :] = block.astype(BF16)
 
+    def fill_part(level, side, h, place):
+        wr = weights[level, side, h, 0].astype(F32).T.astype(BF16)
+        wi = weights[level, side, h, 1].astype(F32).T.astype(BF16)
+        for c, x, value in ((0, 0, wr), (1, 0, -wi), (0, 1, wi), (1, 1, wr)):
+            wide[level, pl.ds((side * 2 + c) * 128, 128), pl.ds((place * 2 + x) * 128, 128)] = value
+
     def fill_wide(level):
         for side in range(2):
             for h in range(2):
-                wr = weights[level, side, h, 0].astype(F32).T.astype(BF16)
-                wi = weights[level, side, h, 1].astype(F32).T.astype(BF16)
-                for c, x, value in ((0, 0, wr), (1, 0, -wi), (0, 1, wi), (1, 1, wr)):
-                    wide[level, pl.ds((side * 2 + c) * 128, 128), pl.ds((h * 2 + x) * 128, 128)] = value
+                fill_part(level, side, h, h)
 
     to_core = pltpu.make_async_remote_copy(
         src_ref=rows_bf.at[1 - core],
@@ -319,17 +326,20 @@
         def _():
             remote(*parts).wait_send()
 
-    for k in range(2):
+    for k in range(CHUNKS):
         level0(*ROWS0[k][0])
-        take_halo(1 - k)
+        if k == 0:
+            take_halo(1)
+        elif k == CHUNKS - 1:
+            take_halo(0)
         level0(*ROWS0[k][1])
         if k == 0:
             pl.when(jnp.logical_not(lower_rng))(lambda: clear1(0))
-        else:
+        elif k == CHUNKS - 1:
             pl.when(jnp.logical_not(upper_rng))(lambda: clear1(rows1 - (margin - RIM)))
         start = CHUNK1[k][0]
         for part in range(2):
-            if k == 1 and part == 0:
+            if k == CHUNKS - 1 and part == 0:
                 rows = hw - start
             else:
                 rows = CHUNK1[k][1]
@@ -341,26 +351,23 @@
                     )
         for i in range(3):
             send_unit(i, k)
-        if k == 0:
-            pl.when(zl == 0)(lambda: send_unit(3, 0))
+        if k < CHUNKS - 1:
+            pl.when(zl == 0)(lambda: send_unit(3, k))
         else:
-            pl.when(zl > 0)(lambda: send_unit(3, 0))
-            send_unit(3, 1)
+            @pl.when(zl > 0)
+            def _():
+                for early in range(CHUNKS - 1):
+                    send_unit(3, early)
+
+            send_unit(3, k)
 
     fill_wide(1)
     fill_table(1)
     fill_wide(2)
     fill_table(2)
     for side in range(2):
-        wr = weights[3, side, core, 0]
-        wi = weights[3, side, core, 1]
-        for c, x, value in ((0, 0, wr), (1, 0, -wi), (0, 1, wi), (1, 1, wr)):
-            wide[3, pl.ds(x * 128, 128), pl.ds((side * 2 + c) * 128, 128)] = value
-    a = lax.broadcasted_iota(jnp.int32, (ANGLES, 128), 0)
-    r = lax.broadcasted_iota(jnp.int32, (ANGLES, 128), 1)
-    phase = ((r * (core * ANGLES + a + 1) * (7 + 3)) % PERIOD).astype(F32) * PHASE_STEP
-    cos_last[...] = jnp.cos(phase)
-    sin_last[...] = jnp.sin(phase)
+        fill_part(3, side, core, 0)
+    fill_phase(3, core, 0)
 
     bits2 = [bits_of(shift_row(2, side)) for side in range(2)]
     bits3 = bits_of(shift_row(3, core))
@@ -377,6 +384,8 @@
 
     def clear(dst, k, margin_rows):
         total = hw + 2 * margin_rows
+        if 0 < k < CHUNKS - 1:
+            return
 
         @pl.when(at_start if k == 0 else at_end)
         def _():
@@ -408,10 +417,10 @@
     def out_copy(i, k):
         start, rows = CHUNK3[k]
         q, own, peer, later = nth_out(i)
-        col = pl.multiple_of(half * hw + start, 128)
+        row = pl.multiple_of(half * hw + start, 64)
         return (
-            turned.at[q, :, :, pl.ds(start, rows)],
-            out.at[:, upper, :, pl.ds(col, rows)],
+            turned.at[q, :, pl.ds(start, rows), :],
+            blocks.at[upper, :, pl.ds(row, rows), :],
             out_send.at[i, k],
             out_recv.at[zl // 2, k],
             peer,
@@ -423,7 +432,7 @@
             pl.when(later)(lambda: pl.semaphore_wait(ready_out.at[q], 1))
         start_copy(out_copy(i, k), own)
 
-    for k in range(2):
+    for k in range(CHUNKS):
         start, rows = CHUNK1[k]
         for s in range(4):
             ref = units.at[s, :, pl.ds(start, rows), :]
@@ -458,17 +467,29 @@
         pair_copy(k).start()
         pair_wait(k).wait_recv()
         for s in range(4):
-            rhs = jnp.concatenate(
+            lhs = jnp.concatenate(
                 [y3[side, s, ch, pl.ds(start, rows), :] for side in range(2) for ch in range(2)], axis=1
             )
-            z = lax.dot_general(
-                wide[3, pl.ds(0, 256), :], rhs, (((1,), (1,)), ((), ())), preferred_element_type=F32
-            )
-            re, im = z[:128], z[128:]
-            turned[s, 0, :, pl.ds(start, rows)] = (re * cos_last[...] - im * sin_last[...]).astype(BF16)
-            turned[s, 1, :, pl.ds(start, rows)] = (re * sin_last[...] + im * cos_last[...]).astype(BF16)
+            merged = jnp.dot(lhs, wide[3, :, pl.ds(0, 256)], preferred_element_type=F32)
+            re, im = turn(3, 0, start % PERIOD, rows, merged[:, :128], merged[:, 128:])
+            turned[s, 0, pl.ds(start, rows), :] = re.astype(BF16)
+            turned[s, 1, pl.ds(start, rows), :] = im.astype(BF16)
         for i in range(4):
             send_block(i, k)
+
+    def block_wait(s, k):
+        start, rows = CHUNK3[k]
+        ref = blocks.at[s // 2, :, pl.ds((s % 2) * hw + start, rows), :]
+        remote(ref, ref, out_send.at[0, k], out_recv.at[s, k], partner).wait_recv()
+
+    for first_chunk, last_chunk, col in ((0, 1, 0), (2, 2, 128)):
+        for s in range(4):
+            for k in range(first_chunk, last_chunk + 1):
+                block_wait(s, k)
+            at = (s % 2) * hw + col
+            for ch in range(2):
+                block = blocks[s // 2, ch, pl.ds(at, 128), :].astype(F32).T
+                out[ch, s // 2, :, pl.ds(at, 128)] = block.astype(BF16)
 
     to_core.wait_send()
     for j in range(2):
@@ -480,23 +501,12 @@
         def _():
             halo_copy(j, 1).wait_send()
 
-    for k in range(2):
+    for k in range(CHUNKS):
         for i in range(4):
             wait_sent(in_copy(i, k), nth(i)[1])
         pair_copy(k).wait_send()
         for i in range(4):
             wait_sent(out_copy(i, k), nth_out(i)[1])
-    for k in range(2):
-        start, rows = CHUNK3[k]
-        for s in range(4):
-            pltpu.make_async_remote_copy(
-                src_ref=turned.at[0, :, :, pl.ds(start, rows)],
-                dst_ref=out.at[:, s // 2, :, pl.ds((s % 2) * hw + start, rows)],
-                send_sem=out_send.at[0, k],
-                recv_sem=out_recv.at[s, k],
-                device_id=partner,
-                device_id_type=MESH,
-            ).wait_recv()
 
 
 def on_device(image, interp_weights, range_taps, range_shifts):
@@ -521,10 +531,8 @@
             pltpu.SMEM(range_taps.shape, F32),
             vmem(range_shifts.shape, jnp.int32),
             vmem((LEVELS, 512, 512), BF16),
-            vmem((3, 2, TABLE, ANGLES), F32),
-            vmem((3, 2, TABLE, ANGLES), F32),
-            vmem((ANGLES, 128), F32),
-            vmem((ANGLES, 128), F32),
+            vmem((LEVELS, 2, TABLE, ANGLES), F32),
+            vmem((LEVELS, 2, TABLE, ANGLES), F32),
             vmem((2, 2, width, ANGLES), BF16),
             vmem((2, 2, width + 2 * margin + 16, ANGLES), F32),
             vmem((2, width, ANGLES), BF16),
@@ -535,17 +543,18 @@
             vmem((4, 2, hw + 4 * RIM + 16, ANGLES), F32),
             vmem((4, 2, hw + 2 * RIM + 16, ANGLES), F32),
             vmem((2, 4, 2, hw, ANGLES), BF16),
-            vmem((4, 2, ANGLES, hw), BF16),
+            vmem((4, 2, hw, ANGLES), BF16),
+            vmem((2, 2, width, ANGLES), BF16),
             dma((4,)),
             dma((2,)),
             dma((2, 2)),
             dma((2, 2)),
-            dma((4, 2)),
-            dma((4, 2)),
-            dma((2,)),
-            dma((2,)),
-            dma((4, 2)),
-            dma((4, 2)),
+            dma((4, CHUNKS)),
+            dma((4, CHUNKS)),
+            dma((CHUNKS,)),
+            dma((CHUNKS,)),
+            dma((4, CHUNKS)),
+            dma((4, CHUNKS)),
             pltpu.SemaphoreType.REGULAR,
             pltpu.SemaphoreType.REGULAR((2,)),
             pltpu.SemaphoreType.REGULAR((4,)),

time: 80.7 us -> 79.5 us (0.985)
  Pallas kernels: 79.8 us -> 78.6 us
    pallas_call x1, Pallas kernels: 79.8 us -> 78.6 us  [on_device(): pl.pallas_call(kernel, out_shape=pltpu.VMEM(image.shape, image.dtype), in...]
where the time goes in v4:
time: 79.5 us; the launch traced here: 79.4 us
  Pallas kernels  78.6 us (99%)
  local copies, waits for them, and re-layouts  0.8 us (1%)
    pallas_call x1, Pallas kernels, on_device(): pl.pallas_call(kernel, out_shape=pltpu.VMEM(image.shape, image.dtype), in...  78.6 us

profile of v4, /device:TPU:65, one launch (start us, length us, event | category | flops | bytes accessed | tf_op | source)
XLA Modules:
  0.0 79.4 jit_solution(3895638165711410928)
XLA Ops:
  0.0 78.6 %backprojection.1 = bf16[2,2,128,512]{3,2,1,0:T(8,128)(2,1)S(1)} custom-call(bf16[2,2,128,512]{3,2,1,0:T(8,128)(2,1)} %image_hbm.1, bf16[4,2,2,2,128,128]{5,4,3,2,1,0:T(8,128)(2,1)} %weights_hbm.1, f32[4,4]{1,0:T(4,128)} %taps_hbm.1, s32[4,2,128]{2,1,0:T(2,128)} %shifts_hbm.1), custom_call_target="tpu_custom_call" | custom-call | tf_op jit(solution)/shard_map/backprojection/pallas_call | solution.py:518
  78.6 0.8 %copy.6 = bf16[2,2,128,512]{3,2,1,0:T(8,128)(2,1)} copy(bf16[2,2,128,512]{3,2,1,0:T(8,128)(2,1)S(1)} %backprojection.1) | data formatting | bytes 1048576

commit v5 on v4

--- a/solution.py
+++ b/solution.py
@@ -282,7 +282,7 @@
     own_bits1 = [((shift_row(1, side0) + RIM) // v) % 2 == 1 for v in (1, 2, 4, 8)]
 
     def nth(i):
-        q = jnp.where(jnp.logical_and(core == 1, zl > 0), i, 3 - i)
+        q = core * i + (1 - core) * (3 - i)
         chip = 4 * core + q
         own = jnp.logical_and(upper == core, quad == q)
         return q, own, device(chip, upper), order(chip, upper) > me
@@ -408,29 +408,21 @@
             device_id=partner, device_id_type=MESH,
         )
 
-    def nth_out(i):
-        q = core * (3 - i) + (1 - core) * i
-        chip = 4 * core + q
-        own = jnp.logical_and(jnp.logical_and(upper == core, side0 == core), quad == q)
-        return q, own, device(chip, side0), order(chip, side0) > me
-
-    def out_copy(i, k):
+    def out_copy(q, k):
         start, rows = CHUNK3[k]
-        q, own, peer, later = nth_out(i)
         row = pl.multiple_of(half * hw + start, 64)
         return (
             turned.at[q, :, pl.ds(start, rows), :],
             blocks.at[upper, :, pl.ds(row, rows), :],
-            out_send.at[i, k],
+            out_send.at[q, k],
             out_recv.at[zl // 2, k],
-            peer,
-        )
-
-    def send_block(i, k):
-        q, own, peer, later = nth_out(i)
+            out_dests[q],
+        )
+
+    def send_block(q, k):
         if k == 0:
-            pl.when(later)(lambda: pl.semaphore_wait(ready_out.at[q], 1))
-        start_copy(out_copy(i, k), own)
+            pl.when(out_later[q])(lambda: pl.semaphore_wait(ready_out.at[q], 1))
+        start_copy(out_copy(q, k), out_self[q])
 
     for k in range(CHUNKS):
         start, rows = CHUNK1[k]
@@ -474,8 +466,10 @@
             re, im = turn(3, 0, start % PERIOD, rows, merged[:, :128], merged[:, 128:])
             turned[s, 0, pl.ds(start, rows), :] = re.astype(BF16)
             turned[s, 1, pl.ds(start, rows), :] = im.astype(BF16)
-        for i in range(4):
-            send_block(i, k)
+        for q in range(3):
+            send_block(q, k)
+    for k in range(CHUNKS):
+        send_block(3, k)
 
     def block_wait(s, k):
         start, rows = CHUNK3[k]
@@ -505,8 +499,8 @@
         for i in range(4):
             wait_sent(in_copy(i, k), nth(i)[1])
         pair_copy(k).wait_send()
-        for i in range(4):
-            wait_sent(out_copy(i, k), nth_out(i)[1])
+        for q in range(4):
+            wait_sent(out_copy(q, k), out_self[q])
 
 
 def on_device(image, interp_weights, range_taps, range_shifts):

time: 79.5 us -> 76.4 us (0.961)
  the two profiles are of different devices: /device:TPU:65 before, /device:TPU:71 now
where the time goes in v5:
time: 76.4 us; the launch traced here: 76.3 us
  Pallas kernels  75.5 us (99%)
  local copies, waits for them, and re-layouts  0.8 us (1%)
    pallas_call x1, Pallas kernels, on_device(): pl.pallas_call(kernel, out_shape=pltpu.VMEM(image.shape, image.dtype), in...  75.5 us

profile of v5, /device:TPU:71, one launch (start us, length us, event | category | flops | bytes accessed | tf_op | source)
XLA Modules:
  0.0 76.3 jit_solution(7713430054208615375)
XLA Ops:
  0.0 75.5 %backprojection.1 = bf16[2,2,128,512]{3,2,1,0:T(8,128)(2,1)S(1)} custom-call(bf16[2,2,128,512]{3,2,1,0:T(8,128)(2,1)} %image_hbm.1, bf16[4,2,2,2,128,128]{5,4,3,2,1,0:T(8,128)(2,1)} %weights_hbm.1, f32[4,4]{1,0:T(4,128)} %taps_hbm.1, s32[4,2,128]{2,1,0:T(2,128)} %shifts_hbm.1), custom_call_target="tpu_custom_call" | custom-call | tf_op jit(solution)/shard_map/backprojection/pallas_call | solution.py:512
  75.5 0.8 %copy.6 = bf16[2,2,128,512]{3,2,1,0:T(8,128)(2,1)} copy(bf16[2,2,128,512]{3,2,1,0:T(8,128)(2,1)S(1)} %backprojection.1) | data formatting | bytes 1048576

commit v6 on v5

--- a/solution.py
+++ b/solution.py
@@ -107,25 +107,30 @@
     for later, own in ((in_later, in_self), (out_later, out_self), (source_later, source_self)):
         for q in range(4):
             count = count + jnp.where(earlier(later[q], own[q]), 1, 0)
-    pl.when(count > 0)(lambda: pl.semaphore_wait(barrier, count))
-
-    @pl.when(upper_rng)
-    def _():
-        for c in range(2):
-            answer(ready_rng.at[core], {"sub": z * 2 + c, "rng": rng + 1})
-
-    @pl.when(core == 0)
-    def _():
-        answer(ready_core, partner)
-
-    for q in range(4):
-        @pl.when(earlier(in_later[q], in_self[q]))
-        def _():
-            answer(ready_in.at[quad], in_peers[q])
-
-        @pl.when(earlier(source_later[q], source_self[q]))
-        def _():
-            answer(ready_out.at[quad], out_sources[q])
+
+    def enter():
+        pl.when(count > 0)(lambda: pl.semaphore_wait(barrier, count))
+
+        @pl.when(upper_rng)
+        def _():
+            for c in range(2):
+                answer(ready_rng.at[core], {"sub": z * 2 + c, "rng": rng + 1})
+
+        @pl.when(core == 0)
+        def _():
+            answer(ready_core, partner)
+
+        for q in range(4):
+            @pl.when(earlier(in_later[q], in_self[q]))
+            def _():
+                answer(ready_in.at[quad], in_peers[q])
+
+            @pl.when(earlier(source_later[q], source_self[q]))
+            def _():
+                answer(ready_out.at[quad], out_sources[q])
+
+    last_to_enter = jnp.logical_and(zl == 0, core == 0)
+    pl.when(last_to_enter)(enter)
 
     def fill_phase(level, h, place):
         r = lax.broadcasted_iota(jnp.int32, (PERIOD, ANGLES), 0)
@@ -147,6 +152,8 @@
             for k in range(width // 128):
                 block = image[ch, j, :, pl.ds(k * 128, 128)].astype(F32).T
                 rows_bf[j, ch, pl.ds(k * 128, 128), :] = block.astype(BF16)
+
+    pl.when(jnp.logical_not(last_to_enter))(enter)
 
     def fill_part(level, side, h, place):
         wr = weights[level, side, h, 0].astype(F32).T.astype(BF16)
@@ -286,6 +293,8 @@
         chip = 4 * core + q
         own = jnp.logical_and(upper == core, quad == q)
         return q, own, device(chip, upper), order(chip, upper) > me
+
+    ahead = jnp.logical_and(core == 1, jnp.logical_and(zl > 0, upper == 0))
 
     def in_copy(i, k):
         start, rows = CHUNK1[k]
@@ -349,15 +358,25 @@
                     y1[h, ch, pl.ds(at, rows), :] = interpolate(
                         lambda o, n: x1[h, ch, pl.ds(at + o, n), :], rows, own_bits1, 1
                     )
-        for i in range(3):
-            send_unit(i, k)
+        @pl.when(jnp.logical_not(ahead))
+        def _():
+            for i in range(3):
+                send_unit(i, k)
+
+        if k == CHUNKS - 1:
+            @pl.when(ahead)
+            def _():
+                for i in range(3):
+                    for each in range(CHUNKS):
+                        send_unit(i, each)
+
         if k < CHUNKS - 1:
             pl.when(zl == 0)(lambda: send_unit(3, k))
         else:
             @pl.when(zl > 0)
             def _():
-                for early in range(CHUNKS - 1):
-                    send_unit(3, early)
+                for each in range(CHUNKS - 1):
+                    send_unit(3, each)
 
             send_unit(3, k)
 

time: 76.4 us -> 75.2 us (0.984)
  the two profiles are of different devices: /device:TPU:71 before, /device:TPU:65 now
where the time goes in v6:
time: 75.2 us; the launch traced here: 74.7 us
  Pallas kernels  73.9 us (98%)
  local copies, waits for them, and re-layouts  0.8 us (1%)
    pallas_call x1, Pallas kernels, on_device(): pl.pallas_call(kernel, out_shape=pltpu.VMEM(image.shape, image.dtype), in...  73.9 us

profile of v6, /device:TPU:65, one launch (start us, length us, event | category | flops | bytes accessed | tf_op | source)
XLA Modules:
  0.0 74.7 jit_solution(15257581949348588199)
XLA Ops:
  0.0 73.9 %backprojection.1 = bf16[2,2,128,512]{3,2,1,0:T(8,128)(2,1)S(1)} custom-call(bf16[2,2,128,512]{3,2,1,0:T(8,128)(2,1)} %image_hbm.1, bf16[4,2,2,2,128,128]{5,4,3,2,1,0:T(8,128)(2,1)} %weights_hbm.1, f32[4,4]{1,0:T(4,128)} %taps_hbm.1, s32[4,2,128]{2,1,0:T(2,128)} %shifts_hbm.1), custom_call_target="tpu_custom_call" | custom-call | tf_op jit(solution)/shard_map/backprojection/pallas_call | solution.py:531
  73.9 0.8 %copy.6 = bf16[2,2,128,512]{3,2,1,0:T(8,128)(2,1)} copy(bf16[2,2,128,512]{3,2,1,0:T(8,128)(2,1)S(1)} %backprojection.1) | data formatting | bytes 1048576

commit v7 on v6

--- a/solution.py
+++ b/solution.py
@@ -18,11 +18,11 @@
 F32 = jnp.float32
 BF16 = jnp.bfloat16
 
-CHUNK1 = ((0, 96), (96, 64), (160, 128))
-CHUNK2 = ((0, 80), (80, 64), (144, 128))
-CHUNK3 = ((0, 64), (64, 64), (128, 128))
+CHUNK1 = ((0, 64), (64, 64), (128, 64), (192, 96))
+CHUNK2 = ((0, 48), (48, 64), (112, 64), (176, 96))
+CHUNK3 = ((0, 32), (32, 64), (96, 64), (160, 96))
 CHUNKS = len(CHUNK3)
-ROWS0 = (((256, 112), (0, 112)), ((112, 64), (368, 64)), ((176, 80), (432, 128)))
+ROWS0 = (((256, 80), (0, 80)), ((80, 64), (336, 64)), ((144, 64), (400, 64)), ((208, 48), (464, 96)))
 TABLE = 256
 
 
@@ -289,7 +289,7 @@
     own_bits1 = [((shift_row(1, side0) + RIM) // v) % 2 == 1 for v in (1, 2, 4, 8)]
 
     def nth(i):
-        q = core * i + (1 - core) * (3 - i)
+        q = jnp.where(jnp.logical_and(core == 1, zl > 0), i, 3 - i)
         chip = 4 * core + q
         own = jnp.logical_and(upper == core, quad == q)
         return q, own, device(chip, upper), order(chip, upper) > me
@@ -429,7 +429,7 @@
 
     def out_copy(q, k):
         start, rows = CHUNK3[k]
-        row = pl.multiple_of(half * hw + start, 64)
+        row = pl.multiple_of(half * hw + start, 32)
         return (
             turned.at[q, :, pl.ds(start, rows), :],
             blocks.at[upper, :, pl.ds(row, rows), :],
@@ -495,7 +495,7 @@
         ref = blocks.at[s // 2, :, pl.ds((s % 2) * hw + start, rows), :]
         remote(ref, ref, out_send.at[0, k], out_recv.at[s, k], partner).wait_recv()
 
-    for first_chunk, last_chunk, col in ((0, 1, 0), (2, 2, 128)):
+    for first_chunk, last_chunk, col in ((0, 2, 0), (3, 3, 128)):
         for s in range(4):
             for k in range(first_chunk, last_chunk + 1):
                 block_wait(s, k)

time: 75.2 us -> 79.4 us (1.056)
  Pallas kernels: 73.9 us -> 78.4 us
    pallas_call x1, Pallas kernels: 73.9 us -> 78.4 us  [on_device(): pl.pallas_call(kernel, out_shape=pltpu.VMEM(image.shape, image.dtype), in...]
where the time goes in v7:
time: 79.4 us; the launch traced here: 79.2 us
  Pallas kernels  78.4 us (99%)
  local copies, waits for them, and re-layouts  0.8 us (1%)
    pallas_call x1, Pallas kernels, on_device(): pl.pallas_call(kernel, out_shape=pltpu.VMEM(image.shape, image.dtype), in...  78.4 us

profile of v7, /device:TPU:65, one launch (start us, length us, event | category | flops | bytes accessed | tf_op | source)
XLA Modules:
  0.0 79.2 jit_solution(6044034590975976419)
XLA Ops:
  0.0 78.4 %backprojection.1 = bf16[2,2,128,512]{3,2,1,0:T(8,128)(2,1)S(1)} custom-call(bf16[2,2,128,512]{3,2,1,0:T(8,128)(2,1)} %image_hbm.1, bf16[4,2,2,2,128,128]{5,4,3,2,1,0:T(8,128)(2,1)} %weights_hbm.1, f32[4,4]{1,0:T(4,128)} %taps_hbm.1, s32[4,2,128]{2,1,0:T(2,128)} %shifts_hbm.1), custom_call_target="tpu_custom_call" | custom-call | tf_op jit(solution)/shard_map/backprojection/pallas_call | solution.py:531
  78.4 0.8 %copy.6 = bf16[2,2,128,512]{3,2,1,0:T(8,128)(2,1)} copy(bf16[2,2,128,512]{3,2,1,0:T(8,128)(2,1)S(1)} %backprojection.1) | data formatting | bytes 1048576

commit v8 on v6

--- a/solution.py
+++ b/solution.py
@@ -47,11 +47,14 @@
     width = image.shape[3]
     hw = width // 2
 
-    load_image = pltpu.make_async_copy(image_hbm, image, load_sem.at[0])
+    def load_image(j, place):
+        return pltpu.make_async_copy(image_hbm.at[:, j], image.at[:, j], load_sem.at[place])
+
     load_weights = pltpu.make_async_copy(weights_hbm, weights, load_sem.at[1])
     load_taps = pltpu.make_async_copy(taps_hbm, taps, load_sem.at[2])
     load_shifts = pltpu.make_async_copy(shifts_hbm, shifts, load_sem.at[3])
-    load_image.start()
+    load_image(1 - core, 0).start()
+    load_image(core, 4).start()
     load_weights.start()
     load_taps.start()
     load_shifts.start()
@@ -145,14 +148,14 @@
         for h in range(2):
             fill_phase(level, h, h)
 
-    load_image.wait()
-
-    for ch in range(2):
-        for j in range(2):
+    def transpose(j):
+        for ch in range(2):
             for k in range(width // 128):
                 block = image[ch, j, :, pl.ds(k * 128, 128)].astype(F32).T
                 rows_bf[j, ch, pl.ds(k * 128, 128), :] = block.astype(BF16)
 
+    load_image(1 - core, 0).wait()
+    transpose(1 - core)
     pl.when(jnp.logical_not(last_to_enter))(enter)
 
     def fill_part(level, side, h, place):
@@ -202,6 +205,8 @@
         pl.semaphore_wait(ready_core, 1)
 
     to_core.start()
+    load_image(core, 4).wait()
+    transpose(core)
 
     @pl.when(upper_rng)
     def _():
@@ -485,10 +490,11 @@
             re, im = turn(3, 0, start % PERIOD, rows, merged[:, :128], merged[:, 128:])
             turned[s, 0, pl.ds(start, rows), :] = re.astype(BF16)
             turned[s, 1, pl.ds(start, rows), :] = im.astype(BF16)
-        for q in range(3):
+        for q in range(2):
             send_block(q, k)
-    for k in range(CHUNKS):
-        send_block(3, k)
+    for q in range(2, 4):
+        for k in range(CHUNKS):
+            send_block(q, k)
 
     def block_wait(s, k):
         start, rows = CHUNK3[k]
@@ -558,7 +564,7 @@
             vmem((2, 4, 2, hw, ANGLES), BF16),
             vmem((4, 2, hw, ANGLES), BF16),
             vmem((2, 2, width, ANGLES), BF16),
-            dma((4,)),
+            dma((5,)),
             dma((2,)),
             dma((2, 2)),
             dma((2, 2)),

time: 75.2 us -> 73.5 us (0.977)
  the two profiles are of different devices: /device:TPU:65 before, /device:TPU:321 now
where the time goes in v8:
time: 73.5 us; the launch traced here: 73.4 us
  Pallas kernels  72.6 us (99%)
  local copies, waits for them, and re-layouts  0.8 us (1%)
    pallas_call x1, Pallas kernels, on_device(): pl.pallas_call(kernel, out_shape=pltpu.VMEM(image.shape, image.dtype), in...  72.6 us

profile of v8, /device:TPU:321, one launch (start us, length us, event | category | flops | bytes accessed | tf_op | source)
XLA Modules:
  0.0 73.4 jit_solution(10320386914024538307)
XLA Ops:
  0.0 72.6 %backprojection.1 = bf16[2,2,128,512]{3,2,1,0:T(8,128)(2,1)S(1)} custom-call(bf16[2,2,128,512]{3,2,1,0:T(8,128)(2,1)} %image_hbm.1, bf16[4,2,2,2,128,128]{5,4,3,2,1,0:T(8,128)(2,1)} %weights_hbm.1, f32[4,4]{1,0:T(4,128)} %taps_hbm.1, s32[4,2,128]{2,1,0:T(2,128)} %shifts_hbm.1), custom_call_target="tpu_custom_call" | custom-call | tf_op jit(solution)/shard_map/backprojection/pallas_call | solution.py:537
  72.6 0.8 %copy.6 = bf16[2,2,128,512]{3,2,1,0:T(8,128)(2,1)} copy(bf16[2,2,128,512]{3,2,1,0:T(8,128)(2,1)S(1)} %backprojection.1) | data formatting | bytes 1048576

commit v9 on v8

--- a/solution.py
+++ b/solution.py
@@ -496,6 +496,23 @@
         for k in range(CHUNKS):
             send_block(q, k)
 
+    to_core.wait_send()
+    for j in range(2):
+        @pl.when(lower_rng)
+        def _():
+            halo_copy(j, 0).wait_send()
+
+        @pl.when(upper_rng)
+        def _():
+            halo_copy(j, 1).wait_send()
+
+    for k in range(CHUNKS):
+        for i in range(4):
+            wait_sent(in_copy(i, k), nth(i)[1])
+        pair_copy(k).wait_send()
+        for q in range(4):
+            wait_sent(out_copy(q, k), out_self[q])
+
     def block_wait(s, k):
         start, rows = CHUNK3[k]
         ref = blocks.at[s // 2, :, pl.ds((s % 2) * hw + start, rows), :]
@@ -509,23 +526,6 @@
             for ch in range(2):
                 block = blocks[s // 2, ch, pl.ds(at, 128), :].astype(F32).T
                 out[ch, s // 2, :, pl.ds(at, 128)] = block.astype(BF16)
-
-    to_core.wait_send()
-    for j in range(2):
-        @pl.when(lower_rng)
-        def _():
-            halo_copy(j, 0).wait_send()
-
-        @pl.when(upper_rng)
-        def _():
-            halo_copy(j, 1).wait_send()
-
-    for k in range(CHUNKS):
-        for i in range(4):
-            wait_sent(in_copy(i, k), nth(i)[1])
-        pair_copy(k).wait_send()
-        for q in range(4):
-            wait_sent(out_copy(q, k), out_self[q])
 
 
 def on_device(image, interp_weights, range_taps, range_shifts):

time: 73.5 us -> 73.5 us (level)
  the two profiles are of different devices: /device:TPU:321 before, /device:TPU:323 now
where the time goes in v9:
time: 73.5 us; the launch traced here: 73.3 us
  Pallas kernels  72.5 us (99%)
  local copies, waits for them, and re-layouts  0.8 us (1%)
    pallas_call x1, Pallas kernels, on_device(): pl.pallas_call(kernel, out_shape=pltpu.VMEM(image.shape, image.dtype), in...  72.5 us

profile of v9, /device:TPU:323, one launch (start us, length us, event | category | flops | bytes accessed | tf_op | source)
XLA Modules:
  0.0 73.3 jit_solution(17279902886077276812)
XLA Ops:
  0.0 72.5 %backprojection.1 = bf16[2,2,128,512]{3,2,1,0:T(8,128)(2,1)S(1)} custom-call(bf16[2,2,128,512]{3,2,1,0:T(8,128)(2,1)} %image_hbm.1, bf16[4,2,2,2,128,128]{5,4,3,2,1,0:T(8,128)(2,1)} %weights_hbm.1, f32[4,4]{1,0:T(4,128)} %taps_hbm.1, s32[4,2,128]{2,1,0:T(2,128)} %shifts_hbm.1), custom_call_target="tpu_custom_call" | custom-call | tf_op jit(solution)/shard_map/backprojection/pallas_call | solution.py:537
  72.5 0.8 %copy.6 = bf16[2,2,128,512]{3,2,1,0:T(8,128)(2,1)} copy(bf16[2,2,128,512]{3,2,1,0:T(8,128)(2,1)S(1)} %backprojection.1) | data formatting | bytes 1048576
